TPU v7x, 512 devices: a whole 4x4x16 slice. The times are simulated.
512 devices in a mesh: blk: 64 (over z, x_lo, core), strip: 8 (over x_hi, y).
Axes of the slice: x: 4 (x_hi: 2, x_lo: 2; x = x_hi * 2 + x_lo), y: 4, z: 16, core: 2. Of those that a mesh axis runs over, the one named last changes fastest.
Arguments:
- points: bfloat16 [81920, 64], P(('blk', 'strip')), may hold values from -6 to 6
- task_ids: int32 [81920], P(('blk', 'strip')), may hold values from 0 to 3
- rhs: bfloat16 [81920, 32], P(('blk', 'strip')), may hold values from -6 to 6
- length_scales: float32 [64], replicated, may hold values from 2 to 5
- coregion: float32 [4, 4], replicated, may hold values from -4 to 6, as said below
- noise: float32 [1], replicated, may hold values from 0.2 to 1
Outputs:
- product: float32 [81920, 32], P(('blk', 'strip'))
Inputs may be any that keep to these rules, and one draw needn't show every extreme that they name: coregion is symmetric positive definite.
All inputs are finite; a program needn't handle non-finite values.
Results may differ from a plain program's by a relative error of at most 0.0041.
Values may be sent and summed in bfloat16 or wider, within the bound.
No kernel may reach another device: no remote copies, remote signals or barrier semaphores. Data moves between devices by JAX's collectives and lax.ppermute only.
A program may use at most 64 MiB of HBM per device.

v0:
```python
import math

import jax
import jax.numpy as jnp
from jax import lax
from jax.sharding import Mesh
from jax.sharding import PartitionSpec as P

BLK_STRIP = ("blk_0", "blk_1", "blk_2", "strip")


def cut_along(value, dim, count):
    before, after = (value.shape[:dim], value.shape[dim + 1 :])
    return jnp.moveaxis(value.reshape(*before, count, -1, *after), dim, 0)


def sent_and_summed(value, axis, dim):
    count = lax.axis_size(axis)
    blocks = lax.all_to_all(cut_along(value, dim, count), axis, 0, 0, tiled=True)
    return jnp.sum(blocks, axis=0)


def side_by_side(arrays, axis, dim, along):
    both = jnp.concatenate(arrays, axis=along)
    whole, at, done = (lax.all_gather(both, axis, axis=dim, tiled=True), 0, [])
    for a in arrays:
        done.append(lax.slice_in_dim(whole, at, at + a.shape[along], axis=along))
        at += a.shape[along]
    return tuple(done)


def from_everyone(value, axis):
    copies = jnp.broadcast_to(value, (lax.axis_size(axis), *value.shape))
    return lax.all_to_all(copies, axis, split_axis=0, concat_axis=0, tiled=True)


def joined_along(blocks, dim):
    blocks = jnp.moveaxis(blocks, 0, dim)
    dims = blocks.shape
    return blocks.reshape(*dims[:dim], dims[dim] * dims[dim + 1], *dims[dim + 2 :])


def gathered_by_axis(value, axes, dim):
    far, near = axes
    blocks = from_everyone(from_everyone(value, far), near)
    return joined_along(blocks.swapaxes(0, 1).reshape(-1, *value.shape), dim)


def side_by_side_2(arrays, axis, dim, along):
    ends, at = ([], 0)
    for a in arrays[:-1]:
        at += a.shape[along]
        ends.append(at)
    both = jnp.concatenate(arrays, axis=along)
    return tuple(jnp.split(gathered_by_axis(both, axis, dim), ends, axis=along))


def scale_points(block_points, length_scales):
    scaled = (block_points.astype(jnp.float32) / length_scales[None, :]).astype(jnp.bfloat16)
    widened = lax.optimization_barrier(scaled).astype(jnp.float32)
    return (scaled, jnp.sum(widened * widened, axis=1))


def task_rows(labels, coregion):
    one_hot = (labels[:, None] == jnp.arange(coregion.shape[0], dtype=jnp.int32)[None, :]).astype(
        jnp.float32
    )
    return jnp.dot(one_hot, coregion, precision=lax.Precision.HIGHEST)


def kernel_tile(row_scaled, row_norms, row_factors, col_scaled, col_norms, col_labels):
    crossed = jnp.einsum("rf,cf->rc", row_scaled, col_scaled, preferred_element_type=jnp.float32)
    squared = jnp.maximum(row_norms[:, None] + col_norms[None, :] - 2.0 * crossed, 0.0)
    radius = jnp.sqrt(5.0 * squared)
    factor = jnp.zeros_like(squared)
    for label_index in range(row_factors.shape[1]):
        factor = jnp.where(
            col_labels[None, :] == label_index, row_factors[:, label_index][:, None], factor
        )
    shaped = (1.0 + radius + radius * radius / 3.0) * jnp.exp(-radius)
    return (factor * shaped).astype(jnp.bfloat16)


def finish(full_sums, rhs, noise):
    summed = sent_and_summed(full_sums, "strip", 0)
    return summed + noise[0] * rhs.astype(jnp.float32)


def body(points, task_ids, rhs, length_scales, coregion, noise):
    block_points, block_rhs, block_labels = (
        *side_by_side((points, rhs), "strip", 0, 1),
        lax.all_gather(task_ids, "strip", axis=0, tiled=True),
    )
    block_scaled, block_norms = scale_points(block_points, length_scales)
    block_factors = task_rows(block_labels, coregion)
    start_sums = jnp.zeros((block_points.shape[0], rhs.shape[1]), jnp.float32)
    piece_points, piece_rhs, piece_labels = (
        *side_by_side_2((points, rhs), (("blk_0", "blk_1"), "blk_2"), 0, 1),
        gathered_by_axis(task_ids, (("blk_0", "blk_1"), "blk_2"), 0),
    )
    count = piece_points.shape[0]
    step = math.gcd(count, 1024)

    def inner(index, acc):
        offset = index * step
        sub_points = lax.dynamic_slice_in_dim(piece_points, offset, step, 0)
        sub_rhs = lax.dynamic_slice_in_dim(piece_rhs, offset, step, 0)
        sub_labels = lax.dynamic_slice_in_dim(piece_labels, offset, step, 0)
        sub_scaled, sub_norms = scale_points(sub_points, length_scales)
        tile = kernel_tile(
            block_scaled, block_norms, block_factors, sub_scaled, sub_norms, sub_labels
        )
        return acc + jnp.dot(tile, sub_rhs, preferred_element_type=jnp.float32)

    block_sums = lax.fori_loop(0, count // step, inner, start_sums)
    return finish(block_sums, rhs, noise)


def solution(mesh):
    finer = Mesh(
        mesh.devices.reshape(16, 2, 2, mesh.shape["strip"]), ("blk_0", "blk_1", "blk_2", "strip")
    )
    placed = (P(BLK_STRIP, None), P(BLK_STRIP), P(BLK_STRIP, None), P(), P(), P())
    return jax.shard_map(
        body, mesh=finer, in_specs=placed, out_specs=P(BLK_STRIP, None), check_vma=False
    )
```

profile of v0, /device:TPU:1, one launch (start us, length us, event | category | flops | bytes accessed | tf_op | source)
XLA Modules:
  0.0 197.6 jit_solution(13081919443251775576)
XLA Ops:
  0.0 1.3 broadcast_in_dim.160
  1.3 16.9 %all-to-all-start = ((s32[32,1,160]{2,1,0:T(1,128)}), s32[32,1,160]{2,1,0:T(1,128)S(1)}, u32[]{:S(2)}, u32[]{:S(2)}) async-start(s32[32,1,160]{2,1,0:T(1,128)} %broadcast_in_dim.160), calls=%async_computation | async-start | bytes 65536 | tf_op jit(solution)/shard_map/all_to_all | solution.py:34
  18.3 0.9 copy.15
  19.2 0.8 copy.16
  20.1 10.4 %all-to-all-done = s32[32,1,160]{2,1,0:T(1,128)S(1)} async-done(((s32[32,1,160]{2,1,0:T(1,128)}), s32[32,1,160]{2,1,0:T(1,128)S(1)}, u32[]{:S(2)}, u32[]{:S(2)}) %all-to-all-start) | async-done | bytes 20512 | tf_op jit(solution)/shard_map/all_to_all | solution.py:34
  30.6 5.5 %all_to_all.29 = s32[2,32,160]{2,1,0:T(8,128)S(1)} all-to-all(s32[2,32,160]{2,1,0:T(8,128)S(1)} %broadcast_in_dim.161), channel_id=1, replica_groups=mesh['blk_0'=16,'blk_1'=2,'blk_2'=2,'strip'=8] {'blk_2'}, dimensions={0} | all-to-all | bytes 81920 | tf_op jit(solution)/shard_map/all_to_all | solution.py:34
  36.1 1.2 broadcast_in_dim.162
  37.3 4.0 %all-to-all-start.2 = ((bf16[32,160,96]{2,1,0:T(8,128)(2,1)}), bf16[32,160,96]{2,1,0:T(8,128)(2,1)S(1)}, u32[]{:S(2)}, u32[]{:S(2)}) async-start(bf16[32,160,96]{2,1,0:T(8,128)(2,1)} %broadcast_in_dim.162), calls=%async_computation.2 | async-start | bytes 2621440 | tf_op jit(solution)/shard_map/all_to_all | solution.py:34
  41.3 30.4 %all_gather.7 = bf16[1280,96]{1,0:T(8,128)(2,1)S(1)} all-gather(bf16[160,96]{1,0:T(8,128)(2,1)S(1)} %pad_maximum_fusion), channel_id=1, replica_groups=mesh['blk_0'=16,'blk_1'=2,'blk_2'=2,'strip'=8] {'strip'}, dimensions={0}, use_global_device_ids=true | all-gather | bytes 276480 | tf_op jit(solution)/shard_map/all_gather | solution.py:25
  71.8 1.3 dynamic-slice
  74.0 10.7 %all-reduce = s32[1280]{0:T(1024)S(1)} all-reduce(s32[1280]{0:T(1024)S(1)} %dynamic-update-slice), channel_id=1, replica_groups=mesh['blk_0'=16,'blk_1'=2,'blk_2'=2,'strip'=8] {'strip'}, use_global_device_ids=true, to_apply=%add | all-reduce | flops 1280 | bytes 10240
  85.0 0.5 fusion.10
  85.7 20.3 %all-to-all-done.2 = bf16[32,160,96]{2,1,0:T(8,128)(2,1)S(1)} async-done(((bf16[32,160,96]{2,1,0:T(8,128)(2,1)}), bf16[32,160,96]{2,1,0:T(8,128)(2,1)S(1)}, u32[]{:S(2)}, u32[]{:S(2)}) %all-to-all-start.2) | async-done | bytes 983072 | tf_op jit(solution)/shard_map/all_to_all | solution.py:34
  105.9 0.3 broadcast_in_dim.163
  106.3 7.3 %all_to_all.30 = bf16[2,32,160,96]{3,2,1,0:T(8,128)(2,1)S(1)} all-to-all(bf16[2,32,160,96]{3,2,1,0:T(8,128)(2,1)S(1)} %broadcast_in_dim.163), channel_id=1, replica_groups=mesh['blk_0'=16,'blk_1'=2,'blk_2'=2,'strip'=8] {'blk_2'}, dimensions={0} | all-to-all | bytes 3932160 | tf_op jit(solution)/shard_map/all_to_all | solution.py:34
  113.6 0.3 copy.17
  113.9 2.0 split.9
  115.8 66.2 %while.14 = (s32[]{:T(128)}, f32[1280,32]{0,1:T(8,128)S(1)}, s32[10240]{0:T(1024)S(1)}, f32[1280,4]{0,1:T(4,128)S(1)}, f32[1280]{0:T(1024)S(1)}, /*index=5*/bf16...) while((s32[]{:T(128)}, f32[1280,32]{0,1:T(8,128)S(1)}, ...), condition=%wide.region_3.4_spmd.clone, body=%wide.region_1.3_spmd.clone.sunk | while | flops 274418688 | bytes 1365441 | solution.py:115
  116.2 6.2 %convolution_add_fusion.2 = f32[1280,32]{0,1:T(8,128)S(1)} fusion(bf16[1024,64]{1,0:T(8,128)(2,1)S(1)} %divide_convert_fusion.3, bf16[1280,64]{1,0:T(8,128)(2,1)S(1)} %get-tuple-element.320, f32[1024]{0:T(1024)S(1)} %multiply_reduce_fusion.3, f32[1280]{0:T(1024)S(1)} %get-tuple-element.317, f32[1280]{0:T(1024)S(1)} %get-tuple-element.279, ...), kind=kOutput, calls=%fused_computation.5.clone.1 | convolution fusion | flops 274022400 | bytes 918533 | tf_op jit(solution)/shard_map/while/body/eval_jaxpr/dot_general | solution.py:113
  122.8 6.2 %convolution_add_fusion.2 = f32[1280,32]{0,1:T(8,128)S(1)} fusion(bf16[1024,64]{1,0:T(8,128)(2,1)S(1)} %divide_convert_fusion.3, bf16[1280,64]{1,0:T(8,128)(2,1)S(1)} %get-tuple-element.320, f32[1024]{0:T(1024)S(1)} %multiply_reduce_fusion.3, f32[1280]{0:T(1024)S(1)} %get-tuple-element.317, f32[1280]{0:T(1024)S(1)} %get-tuple-element.279, ...), kind=kOutput, calls=%fused_computation.5.clone.1 | convolution fusion | flops 274022400 | bytes 918533 | tf_op jit(solution)/shard_map/while/body/eval_jaxpr/dot_general | solution.py:113
  129.5 6.2 %convolution_add_fusion.2 = f32[1280,32]{0,1:T(8,128)S(1)} fusion(bf16[1024,64]{1,0:T(8,128)(2,1)S(1)} %divide_convert_fusion.3, bf16[1280,64]{1,0:T(8,128)(2,1)S(1)} %get-tuple-element.320, f32[1024]{0:T(1024)S(1)} %multiply_reduce_fusion.3, f32[1280]{0:T(1024)S(1)} %get-tuple-element.317, f32[1280]{0:T(1024)S(1)} %get-tuple-element.279, ...), kind=kOutput, calls=%fused_computation.5.clone.1 | convolution fusion | flops 274022400 | bytes 918533 | tf_op jit(solution)/shard_map/while/body/eval_jaxpr/dot_general | solution.py:113
  136.1 6.2 %convolution_add_fusion.2 = f32[1280,32]{0,1:T(8,128)S(1)} fusion(bf16[1024,64]{1,0:T(8,128)(2,1)S(1)} %divide_convert_fusion.3, bf16[1280,64]{1,0:T(8,128)(2,1)S(1)} %get-tuple-element.320, f32[1024]{0:T(1024)S(1)} %multiply_reduce_fusion.3, f32[1280]{0:T(1024)S(1)} %get-tuple-element.317, f32[1280]{0:T(1024)S(1)} %get-tuple-element.279, ...), kind=kOutput, calls=%fused_computation.5.clone.1 | convolution fusion | flops 274022400 | bytes 918533 | tf_op jit(solution)/shard_map/while/body/eval_jaxpr/dot_general | solution.py:113
  142.7 6.2 %convolution_add_fusion.2 = f32[1280,32]{0,1:T(8,128)S(1)} fusion(bf16[1024,64]{1,0:T(8,128)(2,1)S(1)} %divide_convert_fusion.3, bf16[1280,64]{1,0:T(8,128)(2,1)S(1)} %get-tuple-element.320, f32[1024]{0:T(1024)S(1)} %multiply_reduce_fusion.3, f32[1280]{0:T(1024)S(1)} %get-tuple-element.317, f32[1280]{0:T(1024)S(1)} %get-tuple-element.279, ...), kind=kOutput, calls=%fused_computation.5.clone.1 | convolution fusion | flops 274022400 | bytes 918533 | tf_op jit(solution)/shard_map/while/body/eval_jaxpr/dot_general | solution.py:113
  149.3 6.2 %convolution_add_fusion.2 = f32[1280,32]{0,1:T(8,128)S(1)} fusion(bf16[1024,64]{1,0:T(8,128)(2,1)S(1)} %divide_convert_fusion.3, bf16[1280,64]{1,0:T(8,128)(2,1)S(1)} %get-tuple-element.320, f32[1024]{0:T(1024)S(1)} %multiply_reduce_fusion.3, f32[1280]{0:T(1024)S(1)} %get-tuple-element.317, f32[1280]{0:T(1024)S(1)} %get-tuple-element.279, ...), kind=kOutput, calls=%fused_computation.5.clone.1 | convolution fusion | flops 274022400 | bytes 918533 | tf_op jit(solution)/shard_map/while/body/eval_jaxpr/dot_general | solution.py:113
  156.0 6.2 %convolution_add_fusion.2 = f32[1280,32]{0,1:T(8,128)S(1)} fusion(bf16[1024,64]{1,0:T(8,128)(2,1)S(1)} %divide_convert_fusion.3, bf16[1280,64]{1,0:T(8,128)(2,1)S(1)} %get-tuple-element.320, f32[1024]{0:T(1024)S(1)} %multiply_reduce_fusion.3, f32[1280]{0:T(1024)S(1)} %get-tuple-element.317, f32[1280]{0:T(1024)S(1)} %get-tuple-element.279, ...), kind=kOutput, calls=%fused_computation.5.clone.1 | convolution fusion | flops 274022400 | bytes 918533 | tf_op jit(solution)/shard_map/while/body/eval_jaxpr/dot_general | solution.py:113
  162.6 6.2 %convolution_add_fusion.2 = f32[1280,32]{0,1:T(8,128)S(1)} fusion(bf16[1024,64]{1,0:T(8,128)(2,1)S(1)} %divide_convert_fusion.3, bf16[1280,64]{1,0:T(8,128)(2,1)S(1)} %get-tuple-element.320, f32[1024]{0:T(1024)S(1)} %multiply_reduce_fusion.3, f32[1280]{0:T(1024)S(1)} %get-tuple-element.317, f32[1280]{0:T(1024)S(1)} %get-tuple-element.279, ...), kind=kOutput, calls=%fused_computation.5.clone.1 | convolution fusion | flops 274022400 | bytes 918533 | tf_op jit(solution)/shard_map/while/body/eval_jaxpr/dot_general | solution.py:113
  169.2 6.2 %convolution_add_fusion.2 = f32[1280,32]{0,1:T(8,128)S(1)} fusion(bf16[1024,64]{1,0:T(8,128)(2,1)S(1)} %divide_convert_fusion.3, bf16[1280,64]{1,0:T(8,128)(2,1)S(1)} %get-tuple-element.320, f32[1024]{0:T(1024)S(1)} %multiply_reduce_fusion.3, f32[1280]{0:T(1024)S(1)} %get-tuple-element.317, f32[1280]{0:T(1024)S(1)} %get-tuple-element.279, ...), kind=kOutput, calls=%fused_computation.5.clone.1 | convolution fusion | flops 274022400 | bytes 918533 | tf_op jit(solution)/shard_map/while/body/eval_jaxpr/dot_general | solution.py:113
  175.8 6.2 %convolution_add_fusion.2 = f32[1280,32]{0,1:T(8,128)S(1)} fusion(bf16[1024,64]{1,0:T(8,128)(2,1)S(1)} %divide_convert_fusion.3, bf16[1280,64]{1,0:T(8,128)(2,1)S(1)} %get-tuple-element.320, f32[1024]{0:T(1024)S(1)} %multiply_reduce_fusion.3, f32[1280]{0:T(1024)S(1)} %get-tuple-element.317, f32[1280]{0:T(1024)S(1)} %get-tuple-element.279, ...), kind=kOutput, calls=%fused_computation.5.clone.1 | convolution fusion | flops 274022400 | bytes 918533 | tf_op jit(solution)/shard_map/while/body/eval_jaxpr/dot_general | solution.py:113
  182.2 0.8 copy.18
  183.0 6.4 %all-to-all-start.4 = ((f32[8,160,32]{1,2,0:T(8,128)}), f32[8,160,32]{1,2,0:T(8,128)S(1)}, u32[]{:S(2)}, u32[]{:S(2)}) async-start(f32[8,160,32]{1,2,0:T(8,128)} %copy.18), calls=%async_computation.4 | async-start | bytes 524288 | tf_op jit(solution)/shard_map/all_to_all | solution.py:19
  190.0 6.9 %all-to-all-done.4 = f32[8,160,32]{1,2,0:T(8,128)S(1)} async-done(((f32[8,160,32]{1,2,0:T(8,128)}), f32[8,160,32]{1,2,0:T(8,128)S(1)}, u32[]{:S(2)}, u32[]{:S(2)}) %all-to-all-start.4) | async-done | bytes 163872 | tf_op jit(solution)/shard_map/all_to_all | solution.py:19
  197.0 0.6 multiply_add_fusion
  (60 shorter events, 4.5 us)
Async XLA Ops:
  0.0 84.9 %copy-start = (f32[4,4]{1,0:T(4,128)S(1)}, f32[4,4]{1,0:T(4,128)}, u32[]{:S(2)}) copy-start(f32[4,4]{1,0:T(4,128)} %param.12) | copy-start | bytes 196
  0.0 71.7 %copy-start.2 = (f32[64]{0:T(128)S(1)}, f32[64]{0:T(128)}, u32[]{:S(2)}) copy-start(f32[64]{0:T(128)} %param.11) | copy-start | bytes 772
  1.3 29.2 %all-to-all-start = ((s32[32,1,160]{2,1,0:T(1,128)}), s32[32,1,160]{2,1,0:T(1,128)S(1)}, u32[]{:S(2)}, u32[]{:S(2)}) async-start(s32[32,1,160]{2,1,0:T(1,128)} %broadcast_in_dim.160), calls=%async_computation | async-start | bytes 65536 | tf_op jit(solution)/shard_map/all_to_all | solution.py:34
  30.6 43.2 %copy-start.3 = (s32[160]{0:T(256)S(1)}, s32[160]{0:T(256)}, u32[]{:S(2)}) copy-start(s32[160]{0:T(256)} %param.9) | copy-start | bytes 1924
  37.3 68.6 %all-to-all-start.2 = ((bf16[32,160,96]{2,1,0:T(8,128)(2,1)}), bf16[32,160,96]{2,1,0:T(8,128)(2,1)S(1)}, u32[]{:S(2)}, u32[]{:S(2)}) async-start(bf16[32,160,96]{2,1,0:T(8,128)(2,1)} %broadcast_in_dim.162), calls=%async_computation.2 | async-start | bytes 2621440 | tf_op jit(solution)/shard_map/all_to_all | solution.py:34
  115.8 81.2 %copy-start.1 = (bf16[160,32]{0,1:T(8,128)(2,1)S(1)}, bf16[160,32]{0,1:T(8,128)(2,1)}, u32[]{:S(2)}) copy-start(bf16[160,32]{0,1:T(8,128)(2,1)} %param.10) | copy-start | bytes 30724
  183.0 13.9 %all-to-all-start.4 = ((f32[8,160,32]{1,2,0:T(8,128)}), f32[8,160,32]{1,2,0:T(8,128)S(1)}, u32[]{:S(2)}, u32[]{:S(2)}) async-start(f32[8,160,32]{1,2,0:T(8,128)} %copy.18), calls=%async_computation.4 | async-start | bytes 524288 | tf_op jit(solution)/shard_map/all_to_all | solution.py:19
where the time goes:
time: 200 us; the launch traced here: 198 us
  matrix products  62.8 us (31%)
  blocking collectives  53.9 us (27%)
  waiting for transfers between devices  37.6 us (19%)
  starting transfers between devices  27.3 us (14%)
  local copies, waits for them, and re-layouts  10.1 us (5%)
  other arithmetic  3.89 us (2%)
    dot_general x10, matrix products, inner(): return acc + jnp.dot(tile, sub_rhs, preferred_element_type=jnp.float32)  62.2 us
    all_to_all x2, waiting for transfers between devices, from_everyone(): return lax.all_to_all(copies, axis, split_axis=0, concat_axis=0, tiled=True)  30.7 us
    all_gather x1, blocking collectives, side_by_side(): whole, at, done = (lax.all_gather(both, axis, axis=dim, tiled=True), 0, [])  30.4 us
    all_to_all x2, starting transfers between devices, from_everyone(): return lax.all_to_all(copies, axis, split_axis=0, concat_axis=0, tiled=True)  20.9 us
    all_to_all x2, blocking collectives, from_everyone(): return lax.all_to_all(copies, axis, split_axis=0, concat_axis=0, tiled=True)  12.9 us
    unnamed x1, blocking collectives  10.7 us
    all_to_all x1, waiting for transfers between devices, sent_and_summed(): lax.all_to_all(cut_along(value, dim, count), axis, 0, 0, tiled=True)  6.93 us
    all_to_all x1, starting transfers between devices, sent_and_summed(): lax.all_to_all(cut_along(value, dim, count), axis, 0, 0, tiled=True)  6.36 us
  transfers between devices with their start and end apart: 3, of which 3 were waited for; matrix products, arithmetic and copies ran while one was open for 2% of the time, Pallas kernels for 0%

commit v1 on v0

v1 whole, which is shorter than its diff:
```python
import math

import jax
import jax.numpy as jnp
from jax import lax
from jax.experimental import pallas as pl
from jax.experimental.pallas import tpu as pltpu
from jax.sharding import Mesh
from jax.sharding import PartitionSpec as P

FINE = ("zh", "zl", "xl", "core", "xh", "y")
COLS = ("zl", "xh", "xl")
FAR = "zh"
NEAR = ("y", "core")

LANES = 128
ONES = 96
NORMS = 99
TASK = 102

LN2 = math.log(2.0)
SCALE = 5.0 / (LN2 * LN2)
SHIFT = 1.5 / LN2
REST = 0.75 / (LN2 * LN2)
GAIN = LN2 * LN2 / 3.0 * math.exp(1.5)

ROW_STEP = 640
COL_STEP = 256


def split3(value):
    first = value.astype(jnp.bfloat16).astype(jnp.float32)
    left = value - first
    second = left.astype(jnp.bfloat16).astype(jnp.float32)
    third = (left - second).astype(jnp.bfloat16).astype(jnp.float32)
    return first, second, third


def pack_kernel(points, rhs, tasks, scales, rows_out, cols_out):
    count = points.shape[0]
    scaled = (points[...].astype(jnp.float32) / scales[...]).astype(jnp.bfloat16)
    wide = scaled.astype(jnp.float32)
    norms = jnp.sum(wide * wide, axis=1, keepdims=True) * SCALE
    pieces = split3(norms)
    labels = tasks[...].astype(jnp.float32)
    lane = lax.broadcasted_iota(jnp.int32, (count, 32), 1) + 96
    tail_rows = jnp.where(lane < NORMS, 1.0, 0.0)
    tail_cols = jnp.where((lane >= NORMS) & (lane < TASK), 1.0, 0.0)
    for index, piece in enumerate(pieces):
        tail_rows = jnp.where(lane == NORMS + index, piece, tail_rows)
        tail_cols = jnp.where(lane == ONES + index, piece, tail_cols)
    tail_rows = jnp.where(lane == TASK, labels, tail_rows)
    tail_cols = jnp.where(lane == TASK, labels, tail_cols)
    wide_rhs = rhs[...].astype(jnp.float32)
    rows = jnp.concatenate([wide, wide_rhs, tail_rows], axis=1).astype(jnp.bfloat16)
    cols = jnp.concatenate([wide, jnp.zeros_like(wide_rhs), tail_cols], axis=1).astype(jnp.bfloat16)
    for index in range(rows_out.shape[0]):
        rows_out[index] = rows
    for index in range(cols_out.shape[0]):
        cols_out[index] = cols


def pack(points, rhs, task_ids, length_scales, n_rows, n_cols):
    count = points.shape[0]
    return pl.pallas_call(
        pack_kernel,
        out_shape=(
            jax.ShapeDtypeStruct((n_rows, count, LANES), jnp.bfloat16),
            jax.ShapeDtypeStruct((n_cols, count, LANES), jnp.bfloat16),
        ),
        name="pack",
    )(points, rhs, task_ids[:, None], length_scales[None, :])


def shaped(scaled_squared):
    held = jnp.maximum(scaled_squared, 1e-30)
    root = held * lax.rsqrt(held)
    arg = -SHIFT - root
    return ((arg * arg + REST) * jnp.exp2(arg)).astype(jnp.bfloat16)


def tile_kernel(rows, cols, coregion, out, weights, spread, sums, dist_a, dist_b, ker_a, ker_b):
    n_rows, n_cols = rows.shape[0], cols.shape[0]
    n_tasks = coregion.shape[0]
    n_rhs = LANES // n_tasks
    row_blocks, col_blocks = n_rows // ROW_STEP, n_cols // COL_STEP
    steps = row_blocks * col_blocks

    lane = lax.broadcasted_iota(jnp.int32, (1, LANES), 1)
    gains = jnp.where(lane < 64, -2.0 * SCALE, jnp.where((lane >= ONES) & (lane < TASK), 1.0, 0.0))

    def build_weights(index, carry):
        at = pl.multiple_of(index * COL_STEP, COL_STEP)
        value = cols[pl.ds(at, COL_STEP), :].astype(jnp.float32) * gains
        high = value.astype(jnp.bfloat16)
        low = (value - high.astype(jnp.float32)).astype(jnp.bfloat16)
        weights[pl.ds(at, COL_STEP), 0:LANES] = high
        weights[pl.ds(at, COL_STEP), LANES : 2 * LANES] = low
        return carry

    lax.fori_loop(0, col_blocks, build_weights, 0)

    def build_spread(index, carry):
        at = pl.multiple_of(index * LANES, LANES)
        turned = rows[pl.ds(at, LANES), :].astype(jnp.float32).T
        vectors = turned[64 : 64 + n_rhs, :]
        label = turned[TASK : TASK + 1, :]
        parts = [jnp.where(label == float(task), vectors, 0.0) for task in range(n_tasks)]
        spread[:, pl.ds(at, LANES)] = jnp.concatenate(parts, axis=0).astype(jnp.bfloat16)
        return carry

    lax.fori_loop(0, n_rows // LANES, build_spread, 0)

    def places(step):
        block = step // row_blocks
        row = pl.multiple_of((step - block * row_blocks) * ROW_STEP, ROW_STEP)
        return row, pl.multiple_of(block * COL_STEP, COL_STEP)

    def distances(step, dist):
        row, col = places(step)
        left = rows[pl.ds(row, ROW_STEP), :]
        dist[...] = lax.dot_general(
            jnp.concatenate([left, left], axis=1),
            weights[pl.ds(col, COL_STEP), :],
            (((1,), (1,)), ((), ())),
            preferred_element_type=jnp.float32,
        )

    def values(dist, ker):
        ker[...] = shaped(dist[...])

    def product(step, ker):
        row, col = places(step)
        sums[:, pl.ds(col, COL_STEP)] += jnp.dot(
            spread[:, pl.ds(row, ROW_STEP)], ker[...], preferred_element_type=jnp.float32
        )

    sums[...] = jnp.zeros_like(sums)
    distances(0, dist_a)
    distances(1, dist_b)
    values(dist_a, ker_a)

    def pair(index, carry):
        step = index * 2
        distances(step, dist_a)
        values(dist_b, ker_b)
        product(step - 2, ker_a)
        distances(step + 1, dist_b)
        values(dist_a, ker_a)
        product(step - 1, ker_b)
        return carry

    lax.fori_loop(1, steps // 2, pair, 0)
    values(dist_b, ker_b)
    product(steps - 2, ker_a)
    product(steps - 1, ker_b)

    def finish(index, carry):
        at = pl.multiple_of(index * LANES, LANES)
        label = cols[pl.ds(at, LANES), :].astype(jnp.float32).T[TASK : TASK + 1, :]
        total = jnp.zeros((n_rhs, LANES), jnp.float32)
        for task in range(n_tasks):
            factor = jnp.zeros_like(label)
            for own in range(n_tasks):
                factor = jnp.where(label == float(own), coregion[own, task] * GAIN, factor)
            total = total + factor * sums[task * n_rhs : (task + 1) * n_rhs, pl.ds(at, LANES)]
        out[pl.ds(at, LANES), :] = total.T
        return carry

    lax.fori_loop(0, n_cols // LANES, finish, 0)


def tile(rows, cols, coregion):
    n_rows, n_cols = rows.shape[0], cols.shape[0]
    vmem = pl.BlockSpec(memory_space=pltpu.VMEM)
    return pl.pallas_call(
        tile_kernel,
        out_shape=jax.ShapeDtypeStruct((n_cols, LANES // coregion.shape[0]), jnp.float32),
        in_specs=[vmem, vmem, pl.BlockSpec(memory_space=pltpu.SMEM)],
        out_specs=vmem,
        scratch_shapes=[
            pltpu.VMEM((n_cols, 2 * LANES), jnp.bfloat16),
            pltpu.VMEM((LANES, n_rows), jnp.bfloat16),
            pltpu.VMEM((LANES, n_cols), jnp.float32),
            pltpu.VMEM((ROW_STEP, COL_STEP), jnp.float32),
            pltpu.VMEM((ROW_STEP, COL_STEP), jnp.float32),
            pltpu.VMEM((ROW_STEP, COL_STEP), jnp.bfloat16),
            pltpu.VMEM((ROW_STEP, COL_STEP), jnp.bfloat16),
        ],
        name="tile",
    )(rows, cols, coregion)


def exchange(blocks, axes):
    return lax.all_to_all(blocks, axes, 0, 0, tiled=True)


def body(points, task_ids, rhs, length_scales, coregion, noise):
    count, n_rhs = rhs.shape
    far, near, across = (lax.axis_size(axes) for axes in (FAR, NEAR, COLS))
    own_rows, own_cols = pack(points, rhs, task_ids, length_scales, far, across)
    rows = exchange(own_rows, FAR).reshape(far * count, LANES)
    cols = exchange(own_cols, COLS).reshape(across * count, LANES)
    rows = exchange(jnp.broadcast_to(rows, (near,) + rows.shape), NEAR).reshape(-1, LANES)
    partial = tile(rows, cols, coregion)
    back = exchange(partial.reshape(across, count, n_rhs), COLS)
    return jnp.sum(back, axis=0) + noise[0] * rhs.astype(jnp.float32)


def solution(mesh):
    finer = Mesh(mesh.devices.reshape(4, 4, 2, 2, 2, 4), FINE)
    placed = (P(FINE, None), P(FINE), P(FINE, None), P(), P(), P())
    return jax.shard_map(
        body, mesh=finer, in_specs=placed, out_specs=P(FINE, None), check_vma=False
    )
```

time: 200 us -> 145 us (0.72)
  matrix products: 62.8 us -> 0 us
  Pallas kernels: 0 us -> 38.6 us
  blocking collectives: 53.9 us -> 79.3 us
  waiting for transfers between devices: 37.6 us -> 13.1 us
  starting transfers between devices: 27.3 us -> 4.68 us
  other arithmetic: 3.89 us -> 0.66 us
  local copies, waits for them, and re-layouts: 10.1 us -> 7.2 us
    all_to_all x2 -> x3, blocking collectives: 12.9 us -> 79.3 us  [exchange(): return lax.all_to_all(blocks, axes, 0, 0, tiled=True)]
    dot_general x11 -> x0, matrix products: 62.8 us -> none  [the longest x10 62.2 us: inner(): return acc + jnp.dot(tile, sub_rhs, preferred_element_type=jnp.float32)]
    pallas_call x0 -> x2, Pallas kernels: none -> 38.6 us  [the longest x1 36.5 us: tile(): pl.pallas_call(tile_kernel, out_shape=jax.ShapeDtypeStruct((n_cols, LANES...]
    all_gather x1 -> x0, blocking collectives: 30.4 us -> none  [side_by_side(): whole, at, done = (lax.all_gather(both, axis, axis=dim, tiled=True), 0, [])]
    all_to_all x3 -> x1, waiting for transfers between devices: 37.6 us -> 13.1 us  [exchange(): return lax.all_to_all(blocks, axes, 0, 0, tiled=True)]
    all_to_all x3 -> x1, starting transfers between devices: 27.3 us -> 4.68 us  [exchange(): return lax.all_to_all(blocks, axes, 0, 0, tiled=True)]
    unnamed x1 -> x0, blocking collectives: 10.7 us -> none
    reduce_sum x12 -> x1, other arithmetic: 2.36 us -> 0.04 us  [body(): return jnp.sum(back, axis=0) + noise[0] * rhs.astype(jnp.float32)]
  transfers between devices with their start and end apart: 3 -> 1, of which waited for: 3 -> 1; matrix products, arithmetic and copies ran while one was open for 2% -> 0% of each run, Pallas kernels for 0% -> 0%
where the time goes in v1:
time: 145 us; the launch traced here: 144 us
  blocking collectives  79.3 us (55%)
  Pallas kernels  38.6 us (27%)
  waiting for transfers between devices  13.1 us (9%)
  local copies, waits for them, and re-layouts  7.2 us (5%)
  starting transfers between devices  4.68 us (3%)
    all_to_all x3, blocking collectives, exchange(): return lax.all_to_all(blocks, axes, 0, 0, tiled=True)  79.3 us
    pallas_call x1, Pallas kernels, tile(): pl.pallas_call(tile_kernel, out_shape=jax.ShapeDtypeStruct((n_cols, LANES...  36.5 us
    all_to_all x1, waiting for transfers between devices, exchange(): return lax.all_to_all(blocks, axes, 0, 0, tiled=True)  13.1 us
    all_to_all x1, starting transfers between devices, exchange(): return lax.all_to_all(blocks, axes, 0, 0, tiled=True)  4.68 us
    unnamed x6, local copies, waits for them, and re-layouts  2.9 us
  transfers between devices with their start and end apart: 1, of which 1 were waited for; matrix products, arithmetic and copies ran while one was open for 0% of the time, Pallas kernels for 0%

profile of v1, /device:TPU:1, one launch (start us, length us, event | category | flops | bytes accessed | tf_op | source)
XLA Modules:
  0.0 144.2 jit_solution(6510148749057259694)
XLA Ops:
  0.0 1.4 copy.21.tasks
  1.4 1.5 %copy.19.points = bf16[160,64]{1,0:T(8,128)(2,1)} copy(bf16[160,64]{0,1:T(8,128)(2,1)} %param.6) | data formatting | bytes 40960 | tf_op args[0]
  2.9 1.4 copy.20.rhs
  4.3 2.1 %pack.1 = (bf16[4,160,128]{2,1,0:T(8,128)(2,1)}, bf16[16,160,128]{2,1,0:T(8,128)(2,1)}) custom-call(bf16[160,64]{1,0:T(8,128)(2,1)} %copy.19.points, bf16[160,32]{1,0:T(8,128)(2,1)} %copy.20.rhs, s32[160,1]{1,0:T(8,128)} %copy.21.tasks, f32[1,64]{1,0:T(1,128)} %bitcast.13), custom_call_target="tpu_custom_call" | custom-call | tf_op jit(solution)/shard_map/pack/pallas_call | solution.py:65
  6.4 28.6 %all_to_all.20 = bf16[4,160,128]{2,1,0:T(8,128)(2,1)S(1)} all-to-all(bf16[4,160,128]{2,1,0:T(8,128)(2,1)} %get-tuple-element.7), channel_id=1, replica_groups=mesh['zh'=4,'zl'=4,'xl'=2,'core'=2,'xh'=2,'y'=4] {'zh'}, dimensions={0} | all-to-all | bytes 327680 | tf_op jit(solution)/shard_map/all_to_all | solution.py:195
  35.0 0.2 broadcast_in_dim.11
  35.2 0.0 copy-start
  35.2 26.1 %all_to_all.21 = bf16[8,640,128]{2,1,0:T(8,128)(2,1)} all-to-all(bf16[8,640,128]{2,1,0:T(8,128)(2,1)S(1)} %broadcast_in_dim.11), channel_id=1, replica_groups=mesh['zh'=4,'zl'=4,'xl'=2,'core'=2,'xh'=2,'y'=4] {'y','core'}, dimensions={0} | all-to-all | bytes 2621440 | tf_op jit(solution)/shard_map/all_to_all | solution.py:195
  61.3 0.0 copy-done
  61.3 24.6 %all_to_all.22 = bf16[16,160,128]{2,1,0:T(8,128)(2,1)} all-to-all(bf16[16,160,128]{2,1,0:T(8,128)(2,1)S(1)} %copy-done), channel_id=1, replica_groups=mesh['zh'=4,'zl'=4,'xl'=2,'core'=2,'xh'=2,'y'=4] {'zl','xh','xl'}, dimensions={0} | all-to-all | bytes 1310720 | tf_op jit(solution)/shard_map/all_to_all | solution.py:195
  85.9 36.5 %tile.1 = f32[2560,32]{1,0:T(8,128)} custom-call(bf16[5120,128]{1,0:T(8,128)(2,1)} %bitcast.8, bf16[2560,128]{1,0:T(8,128)(2,1)} %bitcast.10, f32[4,4]{1,0:T(4,128)} %coregion.1), custom_call_target="tpu_custom_call" | custom-call | tf_op jit(solution)/shard_map/tile/pallas_call | solution.py:176
  122.4 0.0 copy-start.1
  122.4 2.7 %copy.22 = f32[16,160,32]{1,2,0:T(8,128)} copy(f32[16,160,32]{2,1,0:T(8,128)} %bitcast.9) | data formatting | bytes 655360 | tf_op jit(solution)/shard_map/reshape | solution.py:206
  125.1 4.7 %all-to-all-start.3 = ((f32[16,160,32]{1,2,0:T(8,128)}), f32[16,160,32]{1,2,0:T(8,128)S(1)}, u32[]{:S(2)}, u32[]{:S(2)}) async-start(f32[16,160,32]{1,2,0:T(8,128)} %copy.22), calls=%async_computation.3 | async-start | bytes 1048576 | tf_op jit(solution)/shard_map/all_to_all | solution.py:195
  130.4 13.1 %all-to-all-done.3 = f32[16,160,32]{1,2,0:T(8,128)S(1)} async-done(((f32[16,160,32]{1,2,0:T(8,128)}), f32[16,160,32]{1,2,0:T(8,128)S(1)}, u32[]{:S(2)}, u32[]{:S(2)}) %all-to-all-start.3) | async-done | bytes 327712 | tf_op jit(solution)/shard_map/all_to_all | solution.py:195
  143.5 0.0 copy-done.1
  143.5 0.6 multiply_add_fusion
  (1 shorter events, 0.0 us)
Async XLA Ops:
  35.2 26.1 %copy-start = (bf16[16,160,128]{2,1,0:T(8,128)(2,1)S(1)}, bf16[16,160,128]{2,1,0:T(8,128)(2,1)}, u32[]{:S(2)}) copy-start(bf16[16,160,128]{2,1,0:T(8,128)(2,1)} %get-tuple-element.8) | copy-start | bytes 1966084
  122.4 21.1 %copy-start.1 = (bf16[160,32]{0,1:T(8,128)(2,1)S(1)}, bf16[160,32]{0,1:T(8,128)(2,1)}, u32[]{:S(2)}) copy-start(bf16[160,32]{0,1:T(8,128)(2,1)} %param.8) | copy-start | bytes 30724
  125.1 18.4 %all-to-all-start.3 = ((f32[16,160,32]{1,2,0:T(8,128)}), f32[16,160,32]{1,2,0:T(8,128)S(1)}, u32[]{:S(2)}, u32[]{:S(2)}) async-start(f32[16,160,32]{1,2,0:T(8,128)} %copy.22), calls=%async_computation.3 | async-start | bytes 1048576 | tf_op jit(solution)/shard_map/all_to_all | solution.py:195

commit v2 on v1

v2 whole, which is shorter than its diff:
```python
import math

import jax
import jax.numpy as jnp
from jax import lax
from jax.experimental import pallas as pl
from jax.experimental.pallas import tpu as pltpu
from jax.sharding import Mesh
from jax.sharding import PartitionSpec as P

FINE = ("zh", "zl", "xl", "core", "xh", "y")
COLS = ("zl", "xh", "xl")
FAR = "zh"

LANES = 128
ONES = 96
NORMS = 99
TASK = 102
GROUPS = 4

LN2 = math.log(2.0)
SCALE = 5.0 / (LN2 * LN2)
SHIFT = 1.5 / LN2
REST = 0.75 / (LN2 * LN2)
GAIN = LN2 * LN2 / 3.0 * math.exp(1.5)

ROW_STEP = 5120
COL_STEP = 256

VMEM = pl.BlockSpec(memory_space=pltpu.VMEM)
SMEM = pl.BlockSpec(memory_space=pltpu.SMEM)


def split3(value):
    first = value.astype(jnp.bfloat16).astype(jnp.float32)
    left = value - first
    second = left.astype(jnp.bfloat16).astype(jnp.float32)
    third = (left - second).astype(jnp.bfloat16).astype(jnp.float32)
    return first, second, third


def pack_kernel(at_ref, points, rhs, tasks, scales, rows_out, cols_out):
    count = points.shape[1]
    quarter = count // GROUPS
    wide = (points[...].astype(jnp.float32) / scales[...]).astype(jnp.bfloat16).astype(jnp.float32)
    norms = jnp.sum(wide * wide, axis=0, keepdims=True) * SCALE
    labels = tasks[...].astype(jnp.float32)
    place = lax.broadcasted_iota(jnp.int32, (32, count), 0) + ONES
    tail = jnp.where(place < NORMS, 1.0, 0.0)
    for index, piece in enumerate(split3(norms)):
        tail = jnp.where(place == NORMS + index, piece, tail)
    tail = jnp.where(place == TASK, labels, tail)
    turned = jnp.concatenate([wide, rhs[...].astype(jnp.float32), tail], axis=0).T
    rows = turned.astype(jnp.bfloat16)
    for index in range(rows_out.shape[0]):
        rows_out[index] = rows
    half = count // 2
    features = turned[:, 0:64]
    paired = jnp.concatenate([features[0:half], features[half:count]], axis=1)
    start = lax.rem(at_ref[0] * quarter, LANES)
    lane = lax.broadcasted_iota(jnp.int32, (quarter, 2 * LANES), 1)
    point = lax.broadcasted_iota(jnp.int32, (quarter, 2 * LANES), 0)
    column = turned[:, TASK : TASK + 1]
    lines = []
    for group in range(GROUPS):
        own = column[group * quarter : (group + 1) * quarter]
        line = jnp.sum(jnp.where(lane == point + start, own, 0.0), axis=0, keepdims=True)
        lines += [line[:, 0:LANES], line[:, LANES : 2 * LANES]]
    cols = jnp.concatenate([paired] + lines, axis=0).astype(jnp.bfloat16)
    for index in range(cols_out.shape[0]):
        cols_out[index] = cols


def pack(at, points, rhs, task_ids, length_scales, n_rows, n_cols):
    count = points.shape[1]
    return pl.pallas_call(
        pack_kernel,
        out_shape=(
            jax.ShapeDtypeStruct((n_rows, count, LANES), jnp.bfloat16),
            jax.ShapeDtypeStruct((n_cols, count // 2 + 2 * GROUPS, LANES), jnp.bfloat16),
        ),
        in_specs=[SMEM, VMEM, VMEM, VMEM, VMEM],
        out_specs=(VMEM, VMEM),
        name="pack",
    )(at, points, rhs, task_ids[None, :], length_scales[:, None])


def weigh_kernel(cols, coregion, weights, factors, held, labels):
    pieces = cols.shape[0]
    half = cols.shape[1] - 2 * GROUPS
    quarter = half // 2
    wide = pieces * quarter
    for part in range(2):
        for piece in range(pieces):
            held[part * wide + piece * quarter : part * wide + (piece + 1) * quarter] = cols[
                piece, part * quarter : (part + 1) * quarter
            ].astype(jnp.float32)
    labels[...] = jnp.zeros_like(labels)
    for piece in range(pieces):
        lines = cols[piece, half : half + 2 * GROUPS].astype(jnp.float32)
        tile, spill = divmod(piece * quarter, LANES)
        for group in range(GROUPS):
            at = group * wide + tile * LANES
            labels[:, at : at + LANES] += lines[2 * group : 2 * group + 1]
            if spill + quarter > LANES:
                labels[:, at + LANES : at + 2 * LANES] += lines[2 * group + 1 : 2 * group + 2]
    for task in range(factors.shape[0]):
        factor = jnp.zeros_like(labels)
        for own in range(coregion.shape[0]):
            factor = jnp.where(labels[...] == float(own), coregion[own, task] * GAIN, factor)
        factors[task : task + 1] = factor
    for part in range(2):
        both = held[part * wide : (part + 1) * wide].T
        for side in range(2):
            at = (2 * side + part) * wide
            features = both[side * 64 : (side + 1) * 64]
            norms = jnp.sum(features * features, axis=0, keepdims=True) * SCALE
            value = features * (-2.0 * SCALE)
            high = value.astype(jnp.bfloat16)
            low = (value - high.astype(jnp.float32)).astype(jnp.bfloat16)
            place = lax.broadcasted_iota(jnp.int32, (32, wide), 0) + ONES
            tail = jnp.where((place >= NORMS) & (place < TASK), 1.0, 0.0)
            for index, piece in enumerate(split3(norms)):
                tail = jnp.where(place == ONES + index, piece, tail)
            blank = jnp.zeros((64, wide), jnp.bfloat16)
            weights[0:64, at : at + wide] = high
            weights[64:96, at : at + wide] = blank[0:32]
            weights[96:128, at : at + wide] = tail.astype(jnp.bfloat16)
            weights[128:192, at : at + wide] = low
            weights[192:256, at : at + wide] = blank


def weigh(cols, coregion):
    pieces, height, _ = cols.shape
    total = pieces * (height - 2 * GROUPS) * 2
    return pl.pallas_call(
        weigh_kernel,
        out_shape=(
            jax.ShapeDtypeStruct((2 * LANES, total), jnp.bfloat16),
            jax.ShapeDtypeStruct((coregion.shape[0], total), jnp.float32),
        ),
        in_specs=[VMEM, SMEM],
        out_specs=(VMEM, VMEM),
        scratch_shapes=[
            pltpu.VMEM((total // 2, LANES), jnp.float32),
            pltpu.VMEM((1, total), jnp.float32),
        ],
        name="weigh",
    )(cols, coregion)


def shaped(scaled_squared):
    held = jnp.maximum(scaled_squared, 1e-30)
    root = held * lax.rsqrt(held)
    arg = -SHIFT - root
    return ((arg * arg + REST) * jnp.exp2(arg)).astype(jnp.bfloat16)


def tile_kernel(rows, weights, factors, out, spread, sums, dist_a, dist_b, ker_a, ker_b):
    n_rows, n_cols = rows.shape[0], weights.shape[1]
    n_tasks = factors.shape[0]
    n_rhs = LANES // n_tasks
    row_blocks, col_blocks = n_rows // ROW_STEP, n_cols // COL_STEP
    steps = row_blocks * col_blocks

    def build_spread(index, carry):
        at = pl.multiple_of(index * ROW_STEP, ROW_STEP)
        turned = rows[pl.ds(at, ROW_STEP), :].astype(jnp.float32).T
        vectors = turned[64 : 64 + n_rhs, :]
        label = turned[TASK : TASK + 1, :]
        parts = [jnp.where(label == float(task), vectors, 0.0) for task in range(n_tasks)]
        spread[:, pl.ds(at, ROW_STEP)] = jnp.concatenate(parts, axis=0).astype(jnp.bfloat16)
        return carry

    lax.fori_loop(0, row_blocks, build_spread, 0)

    def places(step):
        block = step // row_blocks
        row = pl.multiple_of((step - block * row_blocks) * ROW_STEP, ROW_STEP)
        return row, pl.multiple_of(block * COL_STEP, COL_STEP)

    sums[...] = jnp.zeros_like(sums)

    def group(index, carry):
        for sub in range(1):
            step = index * 1 + sub
            row, col = places(step)
            left = rows[pl.ds(row, ROW_STEP), :]
            found = jnp.dot(
                jnp.concatenate([left, left], axis=1),
                weights[:, pl.ds(col, COL_STEP)],
                preferred_element_type=jnp.float32,
            )
            sums[:, pl.ds(col, COL_STEP)] += jnp.dot(
                spread[:, pl.ds(row, ROW_STEP)], shaped(found), preferred_element_type=jnp.float32
            )
        return carry

    lax.fori_loop(0, steps // 1, group, 0)
    wide = n_cols // GROUPS
    stacked = []
    for group in range(GROUPS):
        at = group * wide
        total = jnp.zeros((n_rhs, wide), jnp.float32)
        for task in range(n_tasks):
            total = total + (
                factors[task : task + 1, at : at + wide]
                * sums[task * n_rhs : (task + 1) * n_rhs, at : at + wide]
            )
        stacked.append(total)
    out[...] = jnp.concatenate(stacked, axis=0).T


def tile(rows, weights, factors):
    n_rows, n_cols = rows.shape[0], weights.shape[1]
    return pl.pallas_call(
        tile_kernel,
        out_shape=jax.ShapeDtypeStruct((n_cols // GROUPS, LANES), jnp.float32),
        in_specs=[VMEM, VMEM, VMEM],
        out_specs=VMEM,
        scratch_shapes=[
            pltpu.VMEM((LANES, n_rows), jnp.bfloat16),
            pltpu.VMEM((LANES, n_cols), jnp.float32),
            pltpu.VMEM((ROW_STEP, COL_STEP), jnp.float32),
            pltpu.VMEM((ROW_STEP, COL_STEP), jnp.float32),
            pltpu.VMEM((ROW_STEP, COL_STEP), jnp.bfloat16),
            pltpu.VMEM((ROW_STEP, COL_STEP), jnp.bfloat16),
        ],
        name="tile",
    )(rows, weights, factors)


def finish_kernel(parts, rhs, noise, out):
    total = jnp.sum(parts[...], axis=0).T
    n_rhs, _ = rhs.shape
    groups = [total[index * n_rhs : (index + 1) * n_rhs] for index in range(GROUPS)]
    out[...] = jnp.concatenate(groups, axis=1) + noise[0] * rhs[...].astype(jnp.float32)


def finish(parts, rhs, noise):
    return pl.pallas_call(
        finish_kernel,
        out_shape=jax.ShapeDtypeStruct(rhs.shape, jnp.float32),
        in_specs=[VMEM, VMEM, SMEM],
        out_specs=VMEM,
        name="finish",
    )(parts, rhs, noise)


def exchange(blocks, axes):
    return lax.all_to_all(blocks, axes, 0, 0, tiled=True)


def from_all(block, axes):
    return exchange(jnp.broadcast_to(block, (lax.axis_size(axes),) + block.shape), axes)


def body(points, task_ids, rhs, length_scales, coregion, noise):
    far, across = (lax.axis_size(axes) for axes in (FAR, COLS))
    at = lax.axis_index(COLS)[None].astype(jnp.int32)
    own_rows, own_cols = pack(at, points.T, rhs.T, task_ids, length_scales, far, across)
    rows = exchange(own_rows, FAR).reshape(-1, LANES)
    cols = exchange(own_cols, COLS)
    weights, factors = weigh(cols, coregion)
    rows = from_all(rows, "y").reshape(-1, LANES)
    rows = from_all(rows, "core").reshape(-1, LANES)
    partial = tile(rows, weights, factors)
    back = exchange(partial.reshape(across, -1, LANES), COLS)
    return finish(back, rhs.T, noise).T


def solution(mesh):
    finer = Mesh(mesh.devices.reshape(4, 4, 2, 2, 2, 4), FINE)
    placed = (P(FINE, None), P(FINE), P(FINE, None), P(), P(), P())
    return jax.shard_map(
        body, mesh=finer, in_specs=placed, out_specs=P(FINE, None), check_vma=False
    )
```

time: 145 us -> 118 us (0.81)
  blocking collectives: 79.3 us -> 57.2 us
  starting transfers between devices: 4.68 us -> 13.3 us
  Pallas kernels: 38.6 us -> 30.6 us
  local copies, waits for them, and re-layouts: 7.2 us -> 4.37 us
  waiting for transfers between devices: 13.1 us -> 10.9 us
    all_to_all x3, blocking collectives: 79.3 us -> 57.2 us  [exchange(): return lax.all_to_all(blocks, axes, 0, 0, tiled=True)]
    all_to_all x1 -> x2, starting transfers between devices: 4.68 us -> 13.3 us  [exchange(): return lax.all_to_all(blocks, axes, 0, 0, tiled=True)]
    pallas_call x1 -> x3, Pallas kernels: 36.5 us -> 28.8 us  [the longest x1 24.6 us: tile(): pl.pallas_call(tile_kernel, out_shape=jax.ShapeDtypeStruct((n_cols // GRO...]
    reshape x1 -> x0, local copies, waits for them, and re-layouts: 2.7 us -> none  [body(): back = exchange(partial.reshape(across, count, n_rhs), COLS)]
    all_to_all x1 -> x2, waiting for transfers between devices: 13.1 us -> 10.9 us  [exchange(): return lax.all_to_all(blocks, axes, 0, 0, tiled=True)]
  transfers between devices with their start and end apart: 1 -> 2, of which waited for: 1 -> 1; matrix products, arithmetic and copies ran while one was open for 0% -> 0% of each run, Pallas kernels for 0% -> 2%
where the time goes in v2:
time: 118 us; the launch traced here: 117 us
  blocking collectives  57.2 us (48%)
  Pallas kernels  30.6 us (26%)
  starting transfers between devices  13.3 us (11%)
  waiting for transfers between devices  10.9 us (9%)
  local copies, waits for them, and re-layouts  4.37 us (4%)
    all_to_all x3, blocking collectives, exchange(): return lax.all_to_all(blocks, axes, 0, 0, tiled=True)  57.2 us
    pallas_call x1, Pallas kernels, tile(): pl.pallas_call(tile_kernel, out_shape=jax.ShapeDtypeStruct((n_cols // GRO...  24.6 us
    all_to_all x2, starting transfers between devices, exchange(): return lax.all_to_all(blocks, axes, 0, 0, tiled=True)  13.3 us
    all_to_all x2, waiting for transfers between devices, exchange(): return lax.all_to_all(blocks, axes, 0, 0, tiled=True)  10.9 us
    pallas_call x1, Pallas kernels, weigh(): pl.pallas_call(weigh_kernel, out_shape=(jax.ShapeDtypeStruct((2 * LANES,...  2.4 us
  transfers between devices with their start and end apart: 2, of which 1 were waited for; matrix products, arithmetic and copies ran while one was open for 0% of the time, Pallas kernels for 2%

profile of v2, /device:TPU:1, one launch (start us, length us, event | category | flops | bytes accessed | tf_op | source)
XLA Modules:
  0.0 117.0 jit_solution(6312560134306288791)
XLA Ops:
  0.0 1.4 %copy.7.scales = f32[64,1]{1,0:T(8,128)} copy(f32[64,1]{0,1:T(1,128)} %bitcast.18) | data formatting | bytes 512 | tf_op jit(solution)/shard_map/broadcast_in_dim | solution.py:85
  1.4 1.8 %pack.1 = (bf16[4,160,128]{2,1,0:T(8,128)(2,1)}, bf16[16,88,128]{2,1,0:T(8,128)(2,1)}) custom-call(s32[1]{0:T(128)} %bitcast.at_ref, bf16[64,160]{1,0:T(8,128)(2,1)} %bitcast.16, bf16[32,160]{1,0:T(8,128)(2,1)} %bitcast.14, s32[1,160]{1,0:T(1,128)} %bitcast.17, f32[64,1]{1,0:T(8,128)} %copy.7.scales), custom_call_target="tpu_custom_call" | custom-call | tf_op jit(solution)/shard_map/pack/pallas_call | solution.py:76
  3.2 0.0 copy-start.2
  3.2 28.7 %all_to_all.25 = bf16[4,160,128]{2,1,0:T(8,128)(2,1)S(1)} all-to-all(bf16[4,160,128]{2,1,0:T(8,128)(2,1)} %get-tuple-element.9), channel_id=1, replica_groups=mesh['zh'=4,'zl'=4,'xl'=2,'core'=2,'xh'=2,'y'=4] {'zh'}, dimensions={0} | all-to-all | bytes 327680 | tf_op jit(solution)/shard_map/all_to_all | solution.py:251
  31.9 0.1 broadcast_in_dim.18
  32.0 11.6 %all_to_all.26 = bf16[4,640,128]{2,1,0:T(8,128)(2,1)S(1)} all-to-all(bf16[4,640,128]{2,1,0:T(8,128)(2,1)S(1)} %broadcast_in_dim.18), channel_id=1, replica_groups=mesh['zh'=4,'zl'=4,'xl'=2,'core'=2,'xh'=2,'y'=4] {'y'}, dimensions={0} | all-to-all | bytes 1310720 | tf_op jit(solution)/shard_map/all_to_all | solution.py:251
  43.6 0.0 copy-done.2
  43.6 16.8 %all_to_all.27.cols = bf16[16,88,128]{2,1,0:T(8,128)(2,1)} all-to-all(bf16[16,88,128]{2,1,0:T(8,128)(2,1)S(1)} %copy-done.2), channel_id=1, replica_groups=mesh['zh'=4,'zl'=4,'xl'=2,'core'=2,'xh'=2,'y'=4] {'zl','xh','xl'}, dimensions={0} | all-to-all | bytes 720896 | tf_op jit(solution)/shard_map/all_to_all | solution.py:251
  60.4 1.1 broadcast_in_dim.19
  61.6 9.8 %all-to-all-start.2 = ((bf16[2,2560,128]{2,1,0:T(8,128)(2,1)}), bf16[2,2560,128]{2,1,0:T(8,128)(2,1)S(1)}, u32[]{:S(2)}, u32[]{:S(2)}) async-start(bf16[2,2560,128]{2,1,0:T(8,128)(2,1)} %broadcast_in_dim.19), calls=%async_computation.2 | async-start | bytes 2621440 | tf_op jit(solution)/shard_map/all_to_all | solution.py:251
  71.3 2.4 %weigh.1 = (bf16[256,2560]{1,0:T(8,128)(2,1)}, f32[4,2560]{1,0:T(4,128)}) custom-call(bf16[16,88,128]{2,1,0:T(8,128)(2,1)} %all_to_all.27.cols, f32[4,4]{1,0:T(4,128)} %coregion.1), custom_call_target="tpu_custom_call" | custom-call | tf_op jit(solution)/shard_map/weigh/pallas_call | solution.py:136
  73.8 0.0 all-to-all-done.2
  73.8 0.0 copy-start
  73.8 1.1 copy-done
  74.8 24.6 %tile.1 = f32[640,128]{1,0:T(8,128)} custom-call(bf16[5120,128]{1,0:T(8,128)(2,1)} %bitcast.10, bf16[256,2560]{1,0:T(8,128)(2,1)} %get-tuple-element.11.weights, f32[4,2560]{1,0:T(4,128)} %get-tuple-element.12.factors), custom_call_target="tpu_custom_call" | custom-call | tf_op jit(solution)/shard_map/tile/pallas_call | solution.py:216
  99.4 3.5 %all-to-all-start.4 = ((f32[16,40,128]{2,1,0:T(8,128)}), f32[16,40,128]{2,1,0:T(8,128)S(1)}, u32[]{:S(2)}, u32[]{:S(2)}) async-start(f32[16,40,128]{2,1,0:T(8,128)} %bitcast.12), calls=%async_computation.4 | async-start | bytes 655360 | tf_op jit(solution)/shard_map/all_to_all | solution.py:251
  103.6 10.9 %all-to-all-done.4.parts = f32[16,40,128]{2,1,0:T(8,128)S(1)} async-done(((f32[16,40,128]{2,1,0:T(8,128)}), f32[16,40,128]{2,1,0:T(8,128)S(1)}, u32[]{:S(2)}, u32[]{:S(2)}) %all-to-all-start.4) | async-done | bytes 327712 | tf_op jit(solution)/shard_map/all_to_all | solution.py:251
  114.5 0.0 copy-start.1
  114.5 0.7 copy-done.1
  115.2 1.8 %finish.1 = f32[32,160]{1,0:T(8,128)} custom-call(f32[16,40,128]{2,1,0:T(8,128)} %copy-done.1, bf16[32,160]{1,0:T(8,128)(2,1)} %bitcast.15, f32[1]{0:T(128)S(6)} %copy.8.noise), custom_call_target="tpu_custom_call" | custom-call | tf_op jit(solution)/shard_map/finish/pallas_call | solution.py:241
Async XLA Ops:
  3.2 40.4 %copy-start.2 = (bf16[16,88,128]{2,1,0:T(8,128)(2,1)S(1)}, bf16[16,88,128]{2,1,0:T(8,128)(2,1)}, u32[]{:S(2)}) copy-start(bf16[16,88,128]{2,1,0:T(8,128)(2,1)} %get-tuple-element.10) | copy-start | bytes 1081348
  61.6 12.2 %all-to-all-start.2 = ((bf16[2,2560,128]{2,1,0:T(8,128)(2,1)}), bf16[2,2560,128]{2,1,0:T(8,128)(2,1)S(1)}, u32[]{:S(2)}, u32[]{:S(2)}) async-start(bf16[2,2560,128]{2,1,0:T(8,128)(2,1)} %broadcast_in_dim.19), calls=%async_computation.2 | async-start | bytes 2621440 | tf_op jit(solution)/shard_map/all_to_all | solution.py:251
  73.8 1.1 copy-start
  99.4 15.1 %all-to-all-start.4 = ((f32[16,40,128]{2,1,0:T(8,128)}), f32[16,40,128]{2,1,0:T(8,128)S(1)}, u32[]{:S(2)}, u32[]{:S(2)}) async-start(f32[16,40,128]{2,1,0:T(8,128)} %bitcast.12), calls=%async_computation.4 | async-start | bytes 655360 | tf_op jit(solution)/shard_map/all_to_all | solution.py:251
  114.5 0.7 copy-start.1

commit v3 on v2

--- a/solution.py
+++ b/solution.py
@@ -1,3 +1,4 @@
+import functools
 import math
 
 import jax
@@ -9,8 +10,9 @@
 from jax.sharding import PartitionSpec as P
 
 FINE = ("zh", "zl", "xl", "core", "xh", "y")
-COLS = ("zl", "xh", "xl")
+COLS = ("xh", "xl", "y")
 FAR = "zh"
+NEAR = "zl"
 
 LANES = 128
 ONES = 96
@@ -24,8 +26,8 @@
 REST = 0.75 / (LN2 * LN2)
 GAIN = LN2 * LN2 / 3.0 * math.exp(1.5)
 
-ROW_STEP = 5120
 COL_STEP = 256
+
 
 VMEM = pl.BlockSpec(memory_space=pltpu.VMEM)
 SMEM = pl.BlockSpec(memory_space=pltpu.SMEM)
@@ -42,7 +44,8 @@
 def pack_kernel(at_ref, points, rhs, tasks, scales, rows_out, cols_out):
     count = points.shape[1]
     quarter = count // GROUPS
-    wide = (points[...].astype(jnp.float32) / scales[...]).astype(jnp.bfloat16).astype(jnp.float32)
+    column = jnp.broadcast_to(scales[...], (8, scales.shape[1])).T[:, 0:1]
+    wide = (points[...].astype(jnp.float32) / column).astype(jnp.bfloat16).astype(jnp.float32)
     norms = jnp.sum(wide * wide, axis=0, keepdims=True) * SCALE
     labels = tasks[...].astype(jnp.float32)
     place = lax.broadcasted_iota(jnp.int32, (32, count), 0) + ONES
@@ -52,8 +55,7 @@
     tail = jnp.where(place == TASK, labels, tail)
     turned = jnp.concatenate([wide, rhs[...].astype(jnp.float32), tail], axis=0).T
     rows = turned.astype(jnp.bfloat16)
-    for index in range(rows_out.shape[0]):
-        rows_out[index] = rows
+    rows_out[...] = rows
     half = count // 2
     features = turned[:, 0:64]
     paired = jnp.concatenate([features[0:half], features[half:count]], axis=1)
@@ -71,18 +73,18 @@
         cols_out[index] = cols
 
 
-def pack(at, points, rhs, task_ids, length_scales, n_rows, n_cols):
+def pack(at, points, rhs, task_ids, length_scales, n_cols):
     count = points.shape[1]
     return pl.pallas_call(
         pack_kernel,
         out_shape=(
-            jax.ShapeDtypeStruct((n_rows, count, LANES), jnp.bfloat16),
+            jax.ShapeDtypeStruct((count, LANES), jnp.bfloat16),
             jax.ShapeDtypeStruct((n_cols, count // 2 + 2 * GROUPS, LANES), jnp.bfloat16),
         ),
         in_specs=[SMEM, VMEM, VMEM, VMEM, VMEM],
         out_specs=(VMEM, VMEM),
         name="pack",
-    )(at, points, rhs, task_ids[None, :], length_scales[:, None])
+    )(at, points, rhs, task_ids[None, :], length_scales[None, :])
 
 
 def weigh_kernel(cols, coregion, weights, factors, held, labels):
@@ -156,51 +158,46 @@
     return ((arg * arg + REST) * jnp.exp2(arg)).astype(jnp.bfloat16)
 
 
-def tile_kernel(rows, weights, factors, out, spread, sums, dist_a, dist_b, ker_a, ker_b):
-    n_rows, n_cols = rows.shape[0], weights.shape[1]
+def tile_kernel(n_sources, skip_own, unroll, own, *refs):
+    sources, (weights, factors, given, out, held, spread, sums) = refs[:n_sources], refs[n_sources:]
+    n_cols = weights.shape[1]
     n_tasks = factors.shape[0]
     n_rhs = LANES // n_tasks
-    row_blocks, col_blocks = n_rows // ROW_STEP, n_cols // COL_STEP
-    steps = row_blocks * col_blocks
-
-    def build_spread(index, carry):
-        at = pl.multiple_of(index * ROW_STEP, ROW_STEP)
-        turned = rows[pl.ds(at, ROW_STEP), :].astype(jnp.float32).T
-        vectors = turned[64 : 64 + n_rhs, :]
-        label = turned[TASK : TASK + 1, :]
-        parts = [jnp.where(label == float(task), vectors, 0.0) for task in range(n_tasks)]
-        spread[:, pl.ds(at, ROW_STEP)] = jnp.concatenate(parts, axis=0).astype(jnp.bfloat16)
-        return carry
-
-    lax.fori_loop(0, row_blocks, build_spread, 0)
-
-    def places(step):
-        block = step // row_blocks
-        row = pl.multiple_of((step - block * row_blocks) * ROW_STEP, ROW_STEP)
-        return row, pl.multiple_of(block * COL_STEP, COL_STEP)
-
-    sums[...] = jnp.zeros_like(sums)
+
+    at = 0
+    for source in sources:
+        blocks, count, _ = source.shape
+        for index in range(1, blocks) if skip_own else range(blocks):
+            place = lax.rem(own[0] + index, blocks) if skip_own else index
+            held[at : at + count] = source[place]
+            at += count
+
+    turned = held[...].astype(jnp.float32).T
+    vectors = turned[64 : 64 + n_rhs, :]
+    label = turned[TASK : TASK + 1, :]
+    parts = [jnp.where(label == float(task), vectors, 0.0) for task in range(n_tasks)]
+    spread[...] = jnp.concatenate(parts, axis=0).astype(jnp.bfloat16)
 
     def group(index, carry):
-        for sub in range(1):
-            step = index * 1 + sub
-            row, col = places(step)
-            left = rows[pl.ds(row, ROW_STEP), :]
+        for sub in range(unroll):
+            col = pl.multiple_of((index * unroll + sub) * COL_STEP, COL_STEP)
+            left = held[...]
             found = jnp.dot(
                 jnp.concatenate([left, left], axis=1),
                 weights[:, pl.ds(col, COL_STEP)],
                 preferred_element_type=jnp.float32,
             )
-            sums[:, pl.ds(col, COL_STEP)] += jnp.dot(
-                spread[:, pl.ds(row, ROW_STEP)], shaped(found), preferred_element_type=jnp.float32
+            sums[:, pl.ds(col, COL_STEP)] = jnp.dot(
+                spread[...], shaped(found), preferred_element_type=jnp.float32
             )
         return carry
 
-    lax.fori_loop(0, steps // 1, group, 0)
+    lax.fori_loop(0, n_cols // COL_STEP // unroll, group, 0)
+
     wide = n_cols // GROUPS
     stacked = []
-    for group in range(GROUPS):
-        at = group * wide
+    for index in range(GROUPS):
+        at = index * wide
         total = jnp.zeros((n_rhs, wide), jnp.float32)
         for task in range(n_tasks):
             total = total + (
@@ -208,26 +205,23 @@
                 * sums[task * n_rhs : (task + 1) * n_rhs, at : at + wide]
             )
         stacked.append(total)
-    out[...] = jnp.concatenate(stacked, axis=0).T
-
-
-def tile(rows, weights, factors):
-    n_rows, n_cols = rows.shape[0], weights.shape[1]
-    return pl.pallas_call(
-        tile_kernel,
+    out[...] = jnp.concatenate(stacked, axis=0).T + given[...]
+
+
+def tile(sources, own, weights, factors, given, skip_own, unroll):
+    n_cols = weights.shape[1]
+    n_rows = sum((s.shape[0] - (1 if skip_own else 0)) * s.shape[1] for s in sources)
+    return pl.pallas_call(
+        functools.partial(tile_kernel, len(sources), skip_own, unroll),
         out_shape=jax.ShapeDtypeStruct((n_cols // GROUPS, LANES), jnp.float32),
-        in_specs=[VMEM, VMEM, VMEM],
+        in_specs=[SMEM] + [VMEM] * (len(sources) + 3),
         out_specs=VMEM,
         scratch_shapes=[
+            pltpu.VMEM((n_rows, LANES), jnp.bfloat16),
             pltpu.VMEM((LANES, n_rows), jnp.bfloat16),
             pltpu.VMEM((LANES, n_cols), jnp.float32),
-            pltpu.VMEM((ROW_STEP, COL_STEP), jnp.float32),
-            pltpu.VMEM((ROW_STEP, COL_STEP), jnp.float32),
-            pltpu.VMEM((ROW_STEP, COL_STEP), jnp.bfloat16),
-            pltpu.VMEM((ROW_STEP, COL_STEP), jnp.bfloat16),
         ],
-        name="tile",
-    )(rows, weights, factors)
+    )(own, *sources, weights, factors, given)
 
 
 def finish_kernel(parts, rhs, noise, out):
@@ -251,21 +245,30 @@
     return lax.all_to_all(blocks, axes, 0, 0, tiled=True)
 
 
-def from_all(block, axes):
-    return exchange(jnp.broadcast_to(block, (lax.axis_size(axes),) + block.shape), axes)
+def from_shift(value, axis, shift):
+    count = lax.axis_size(axis)
+    return lax.ppermute(value, axis, [(i, (i + shift) % count) for i in range(count)])
 
 
 def body(points, task_ids, rhs, length_scales, coregion, noise):
-    far, across = (lax.axis_size(axes) for axes in (FAR, COLS))
+    far, near, across = (lax.axis_size(axes) for axes in (FAR, NEAR, COLS))
     at = lax.axis_index(COLS)[None].astype(jnp.int32)
-    own_rows, own_cols = pack(at, points.T, rhs.T, task_ids, length_scales, far, across)
-    rows = exchange(own_rows, FAR).reshape(-1, LANES)
+    own = lax.axis_index(NEAR)[None].astype(jnp.int32)
+    own_rows, own_cols = pack(at, points.T, rhs.T, task_ids, length_scales, across)
+    others = [from_shift(own_rows, FAR, shift) for shift in (far // 2, 1, far - 1)]
     cols = exchange(own_cols, COLS)
+    rows = jnp.stack([own_rows] + others)
+    twin = from_shift(rows, "core", 1)
+    rows = rows.reshape(1, -1, LANES)
+    all_rows = exchange(jnp.broadcast_to(rows, (near,) + rows.shape[1:]), NEAR)
     weights, factors = weigh(cols, coregion)
-    rows = from_all(rows, "y").reshape(-1, LANES)
-    rows = from_all(rows, "core").reshape(-1, LANES)
-    partial = tile(rows, weights, factors)
-    back = exchange(partial.reshape(across, -1, LANES), COLS)
+    empty = jnp.zeros((weights.shape[1] // GROUPS, LANES), jnp.float32)
+    first = (rows, twin.reshape(rows.shape))
+    total = tile(first, own, weights, factors, empty, False, 5)
+    twins = from_shift(all_rows, "core", 1)
+    total = tile((all_rows,), own, weights, factors, total, True, 2)
+    total = tile((twins,), own, weights, factors, total, True, 2)
+    back = exchange(total.reshape(across, -1, LANES), COLS)
     return finish(back, rhs.T, noise).T
 
 

time: 118 us -> 122 us (1.034)
  blocking collectives: 57.2 us -> 20.3 us
  starting transfers between devices: 13.3 us -> 42.1 us
  waiting for transfers between devices: 10.9 us -> 17.5 us
  Pallas kernels: 30.6 us -> 37.1 us
    all_to_all x3 -> x1, blocking collectives: 57.2 us -> 20.3 us  [exchange(): return lax.all_to_all(blocks, axes, 0, 0, tiled=True)]
    ppermute x0 -> x5, starting transfers between devices: none -> 31.4 us  [from_shift(): lax.ppermute(value, axis, [(i, (i + shift) % count) for i in range(count)])]
    pallas_call x2 -> x4, Pallas kernels: 26.4 us -> 32.9 us  [the longest x3 31 us: tile(): pl.pallas_call(functools.partial(tile_kernel, len(sources), skip_own, unr...]
    ppermute x0 -> x5, waiting for transfers between devices: none -> 3.68 us  [from_shift(): lax.ppermute(value, axis, [(i, (i + shift) % count) for i in range(count)])]
    all_to_all x2, waiting for transfers between devices: 10.9 us -> 13.8 us  [exchange(): return lax.all_to_all(blocks, axes, 0, 0, tiled=True)]
    all_to_all x2, starting transfers between devices: 13.3 us -> 10.7 us  [exchange(): return lax.all_to_all(blocks, axes, 0, 0, tiled=True)]
    broadcast_in_dim x3 -> x2, local copies, waits for them, and re-layouts: 2.59 us -> 0.88 us  [the longest x1 0.79 us: body(): empty = jnp.zeros((weights.shape[1] // GROUPS, LANES), jnp.float32)]
  transfers between devices with their start and end apart: 2 -> 7, of which waited for: 1 -> 4; matrix products, arithmetic and copies ran while one was open for 0% -> 1% of each run, Pallas kernels for 2% -> 18%
where the time goes in v3:
time: 122 us
  starting transfers between devices  42.1 us (35%)
  Pallas kernels  37.1 us (30%)
  blocking collectives  20.3 us (17%)
  waiting for transfers between devices  17.5 us (14%)
  local copies, waits for them, and re-layouts  3.19 us (3%)
    ppermute x5, starting transfers between devices, from_shift(): lax.ppermute(value, axis, [(i, (i + shift) % count) for i in range(count)])  31.4 us
    pallas_call x3, Pallas kernels, tile(): pl.pallas_call(functools.partial(tile_kernel, len(sources), skip_own, unr...  31 us
    all_to_all x1, blocking collectives, exchange(): return lax.all_to_all(blocks, axes, 0, 0, tiled=True)  20.3 us
    all_to_all x2, waiting for transfers between devices, exchange(): return lax.all_to_all(blocks, axes, 0, 0, tiled=True)  13.8 us
    all_to_all x2, starting transfers between devices, exchange(): return lax.all_to_all(blocks, axes, 0, 0, tiled=True)  10.7 us
    ppermute x5, waiting for transfers between devices, from_shift(): lax.ppermute(value, axis, [(i, (i + shift) % count) for i in range(count)])  3.68 us
  transfers between devices with their start and end apart: 7, of which 4 were waited for; matrix products, arithmetic and copies ran while one was open for 1% of the time, Pallas kernels for 18%

profile of v3, /device:TPU:1, one launch (start us, length us, event | category | flops | bytes accessed | tf_op | source)
XLA Modules:
  0.0 121.6 jit_solution(13034468022514816568)
XLA Ops:
  0.0 1.9 %pack.1 = (bf16[160,128]{1,0:T(8,128)(2,1)}, bf16[16,88,128]{2,1,0:T(8,128)(2,1)}) custom-call(s32[1]{0:T(128)} %bitcast.1.at_ref, bf16[64,160]{1,0:T(8,128)(2,1)} %bitcast.25, bf16[32,160]{1,0:T(8,128)(2,1)} %bitcast.19, s32[1,160]{1,0:T(1,128)} %bitcast.26, f32[1,64]{1,0:T(1,128)} %bitcast.27), custom_call_target="tpu_custom_call" | custom-call | tf_op jit(solution)/shard_map/pack/pallas_call | solution.py:78
  1.9 16.2 %collective-permute-start = (bf16[160,128]{1,0:T(8,128)(2,1)}, bf16[160,128]{1,0:T(8,128)(2,1)S(1)}, u32[]{:S(2)}, u32[]{:S(2)}) collective-permute-start(bf16[160,128]{1,0:T(8,128)(2,1)} %get-tuple-element.9), channel_id=1, source_target_pairs={{0,256},{128,384},{256,0},{384,128},{1,257},{129,385},{257,1},{385... | collective-permute-start | bytes 122888 | tf_op jit(solution)/shard_map/ppermute | solution.py:250
  18.1 4.0 %collective-permute-start.1 = (bf16[160,128]{1,0:T(8,128)(2,1)}, bf16[160,128]{1,0:T(8,128)(2,1)S(1)}, u32[]{:S(2)}, u32[]{:S(2)}) collective-permute-start(bf16[160,128]{1,0:T(8,128)(2,1)} %get-tuple-element.9), channel_id=1, source_target_pairs={{0,128},{128,256},{256,384},{384,0},{1,129},{129,257},{257,385},{3... | collective-permute-start | bytes 122888 | tf_op jit(solution)/shard_map/ppermute | solution.py:250
  22.1 5.2 %collective-permute-start.2 = (bf16[160,128]{1,0:T(8,128)(2,1)}, bf16[160,128]{1,0:T(8,128)(2,1)S(1)}, u32[]{:S(2)}, u32[]{:S(2)}) collective-permute-start(bf16[160,128]{1,0:T(8,128)(2,1)} %get-tuple-element.9), channel_id=1, source_target_pairs={{0,384},{128,0},{256,128},{384,256},{1,385},{129,1},{257,129},{385... | collective-permute-start | bytes 122888 | tf_op jit(solution)/shard_map/ppermute | solution.py:250
  27.3 0.0 collective-permute-done
  27.3 0.4 collective-permute-done.1
  27.7 3.3 %collective-permute-done.2 = bf16[160,128]{1,0:T(8,128)(2,1)S(1)} collective-permute-done((bf16[160,128]{1,0:T(8,128)(2,1)}, bf16[160,128]{1,0:T(8,128)(2,1)S(1)}, u32[]{:S(2)}, u32[]{:S(2)}) %collective-permute-start.2) | collective-permute-done | bytes 40992 | tf_op jit(solution)/shard_map/ppermute | solution.py:250
  31.0 0.8 pad_maximum_fusion
  31.8 0.0 copy-start.1
  31.8 0.1 broadcast_in_dim.27
  31.9 20.3 %all_to_all.15.refs_0_ = bf16[4,640,128]{2,1,0:T(8,128)(2,1)S(1)} all-to-all(bf16[4,640,128]{2,1,0:T(8,128)(2,1)S(1)} %broadcast_in_dim.27), channel_id=1, replica_groups=mesh['zh'=4,'zl'=4,'xl'=2,'core'=2,'xh'=2,'y'=4] {'zl'}, dimensions={0} | all-to-all | bytes 1310720 | tf_op jit(solution)/shard_map/all_to_all | solution.py:245
  52.2 0.0 copy-start
  52.2 3.8 %collective-permute-start.3 = (bf16[4,640,128]{2,1,0:T(8,128)(2,1)S(1)}, bf16[4,640,128]{2,1,0:T(8,128)(2,1)S(1)}, u32[]{:S(2)}, u32[]{:S(2)}) collective-permute-start(bf16[4,640,128]{2,1,0:T(8,128)(2,1)S(1)} %all_to_all.15.refs_0_), channel_id=1, source_target_pairs={{0,8},{8,0},{1,9},{9,1},{2,10},{10,2},{3,11},{11,3},{4,12},{12,4},... | collective-permute-start | bytes 1966088 | tf_op jit(solution)/shard_map/ppermute | solution.py:250
  56.0 6.7 %all-to-all-start.1 = ((bf16[16,88,128]{2,1,0:T(8,128)(2,1)}), bf16[16,88,128]{2,1,0:T(8,128)(2,1)S(1)}, u32[]{:S(2)}, u32[]{:S(2)}) async-start(bf16[16,88,128]{2,1,0:T(8,128)(2,1)} %get-tuple-element.10), calls=%async_computation.1 | async-start | bytes 720896 | tf_op jit(solution)/shard_map/all_to_all | solution.py:245
  62.7 0.0 copy-done.1
  62.7 2.2 %collective-permute-start.4 = (bf16[4,160,128]{2,1,0:T(8,128)(2,1)S(1)}, bf16[4,160,128]{2,1,0:T(8,128)(2,1)S(1)}, u32[]{:S(2)}, u32[]{:S(2)}) collective-permute-start(bf16[4,160,128]{2,1,0:T(8,128)(2,1)S(1)} %pad_maximum_fusion), channel_id=1, source_target_pairs={{0,8},{8,0},{1,9},{9,1},{2,10},{10,2},{3,11},{11,3},{4,12},{12,4},... | collective-permute-start | bytes 491528 | tf_op jit(solution)/shard_map/ppermute | solution.py:250
  64.9 6.6 %all-to-all-done.1.cols = bf16[16,88,128]{2,1,0:T(8,128)(2,1)S(1)} async-done(((bf16[16,88,128]{2,1,0:T(8,128)(2,1)}), bf16[16,88,128]{2,1,0:T(8,128)(2,1)S(1)}, u32[]{:S(2)}, u32[]{:S(2)}) %all-to-all-start.1) | async-done | bytes 360480 | tf_op jit(solution)/shard_map/all_to_all | solution.py:245
  71.5 0.7 copy-done.2
  72.2 2.4 %weigh.1 = (bf16[256,2560]{1,0:T(8,128)(2,1)}, f32[4,2560]{1,0:T(4,128)}) custom-call(bf16[16,88,128]{2,1,0:T(8,128)(2,1)} %copy-done.2, f32[4,4]{1,0:T(4,128)} %coregion.1), custom_call_target="tpu_custom_call" | custom-call | tf_op jit(solution)/shard_map/weigh/pallas_call | solution.py:138
  74.6 0.0 collective-permute-done.4
  74.6 0.8 broadcast_in_dim.28.refs_4_
  75.4 0.0 copy-done.5
  75.4 8.5 %shard_map.64.refs_3_ = f32[640,128]{1,0:T(8,128)} custom-call(s32[1]{0:T(128)} %bitcast.own, bf16[1,640,128]{2,1,0:T(8,128)(2,1)} %bitcast.16, bf16[1,640,128]{2,1,0:T(8,128)(2,1)} %bitcast.18, bf16[256,2560]{1,0:T(8,128)(2,1)} %get-tuple-element.11.refs_2_.refs_1_, f32[4,2560]{1,0:T(4,128)} %get-tuple-element.12.refs_3_.refs_2_, ...), custom_call_target="tpu_custom_call" | custom-call | tf_op jit(solution)/shard_map/pallas_call | solution.py:214
  84.0 0.0 copy-done
  84.0 11.2 %shard_map.65.refs_3_ = f32[640,128]{1,0:T(8,128)} custom-call(s32[1]{0:T(128)} %bitcast.own, bf16[4,640,128]{2,1,0:T(8,128)(2,1)} %copy-done, bf16[256,2560]{1,0:T(8,128)(2,1)} %get-tuple-element.11.refs_2_.refs_1_, f32[4,2560]{1,0:T(4,128)} %get-tuple-element.12.refs_3_.refs_2_, f32[640,128]{1,0:T(8,128)} %shard_map.64.refs_3_), custom_call_target="tpu_custom_call" | custom-call | tf_op jit(solution)/shard_map/pallas_call | solution.py:214
  95.2 0.0 collective-permute-done.3.refs_0_
  95.2 0.8 copy-done.4
  96.1 11.3 %shard_map.66 = f32[640,128]{1,0:T(8,128)} custom-call(s32[1]{0:T(128)} %bitcast.own, bf16[4,640,128]{2,1,0:T(8,128)(2,1)} %copy-done.4, bf16[256,2560]{1,0:T(8,128)(2,1)} %get-tuple-element.11.refs_2_.refs_1_, f32[4,2560]{1,0:T(4,128)} %get-tuple-element.12.refs_3_.refs_2_, f32[640,128]{1,0:T(8,128)} %shard_map.65.refs_3_), custom_call_target="tpu_custom_call" | custom-call | tf_op jit(solution)/shard_map/pallas_call | solution.py:214
  107.3 3.9 %all-to-all-start.2 = ((f32[16,40,128]{2,1,0:T(8,128)}), f32[16,40,128]{2,1,0:T(8,128)S(1)}, u32[]{:S(2)}, u32[]{:S(2)}) async-start(f32[16,40,128]{2,1,0:T(8,128)} %bitcast.17), calls=%async_computation.2 | async-start | bytes 655360 | tf_op jit(solution)/shard_map/all_to_all | solution.py:245
  111.9 7.2 %all-to-all-done.2.parts = f32[16,40,128]{2,1,0:T(8,128)S(1)} async-done(((f32[16,40,128]{2,1,0:T(8,128)}), f32[16,40,128]{2,1,0:T(8,128)S(1)}, u32[]{:S(2)}, u32[]{:S(2)}) %all-to-all-start.2) | async-done | bytes 327712 | tf_op jit(solution)/shard_map/all_to_all | solution.py:245
  119.1 0.7 copy-done.3
  119.8 1.8 %finish.1 = f32[32,160]{1,0:T(8,128)} custom-call(f32[16,40,128]{2,1,0:T(8,128)} %copy-done.3, bf16[32,160]{1,0:T(8,128)(2,1)} %bitcast.20, f32[1]{0:T(128)S(6)} %copy.7.noise), custom_call_target="tpu_custom_call" | custom-call | tf_op jit(solution)/shard_map/finish/pallas_call | solution.py:235
  (4 shorter events, 0.0 us)
Async XLA Ops:
  1.9 25.5 %collective-permute-start = (bf16[160,128]{1,0:T(8,128)(2,1)}, bf16[160,128]{1,0:T(8,128)(2,1)S(1)}, u32[]{:S(2)}, u32[]{:S(2)}) collective-permute-start(bf16[160,128]{1,0:T(8,128)(2,1)} %get-tuple-element.9), channel_id=1, source_target_pairs={{0,256},{128,384},{256,0},{384,128},{1,257},{129,385},{257,1},{385... | collective-permute-start | bytes 122888 | tf_op jit(solution)/shard_map/ppermute | solution.py:250
  18.1 9.6 %collective-permute-start.1 = (bf16[160,128]{1,0:T(8,128)(2,1)}, bf16[160,128]{1,0:T(8,128)(2,1)S(1)}, u32[]{:S(2)}, u32[]{:S(2)}) collective-permute-start(bf16[160,128]{1,0:T(8,128)(2,1)} %get-tuple-element.9), channel_id=1, source_target_pairs={{0,128},{128,256},{256,384},{384,0},{1,129},{129,257},{257,385},{3... | collective-permute-start | bytes 122888 | tf_op jit(solution)/shard_map/ppermute | solution.py:250
  22.1 8.9 %collective-permute-start.2 = (bf16[160,128]{1,0:T(8,128)(2,1)}, bf16[160,128]{1,0:T(8,128)(2,1)S(1)}, u32[]{:S(2)}, u32[]{:S(2)}) collective-permute-start(bf16[160,128]{1,0:T(8,128)(2,1)} %get-tuple-element.9), channel_id=1, source_target_pairs={{0,384},{128,0},{256,128},{384,256},{1,385},{129,1},{257,129},{385... | collective-permute-start | bytes 122888 | tf_op jit(solution)/shard_map/ppermute | solution.py:250
  31.8 30.9 %copy-start.1 = (bf16[4,160,128]{2,1,0:T(8,128)(2,1)}, bf16[4,160,128]{2,1,0:T(8,128)(2,1)S(1)}, u32[]{:S(2)}) copy-start(bf16[4,160,128]{2,1,0:T(8,128)(2,1)S(1)} %pad_maximum_fusion) | copy-start | bytes 491524
  52.2 31.8 %copy-start = (bf16[4,640,128]{2,1,0:T(8,128)(2,1)}, bf16[4,640,128]{2,1,0:T(8,128)(2,1)S(1)}, u32[]{:S(2)}) copy-start(bf16[4,640,128]{2,1,0:T(8,128)(2,1)S(1)} %all_to_all.15.refs_0_) | copy-start | bytes 1966084
  52.2 43.0 %collective-permute-start.3 = (bf16[4,640,128]{2,1,0:T(8,128)(2,1)S(1)}, bf16[4,640,128]{2,1,0:T(8,128)(2,1)S(1)}, u32[]{:S(2)}, u32[]{:S(2)}) collective-permute-start(bf16[4,640,128]{2,1,0:T(8,128)(2,1)S(1)} %all_to_all.15.refs_0_), channel_id=1, source_target_pairs={{0,8},{8,0},{1,9},{9,1},{2,10},{10,2},{3,11},{11,3},{4,12},{12,4},... | collective-permute-start | bytes 1966088 | tf_op jit(solution)/shard_map/ppermute | solution.py:250
  56.0 15.5 %all-to-all-start.1 = ((bf16[16,88,128]{2,1,0:T(8,128)(2,1)}), bf16[16,88,128]{2,1,0:T(8,128)(2,1)S(1)}, u32[]{:S(2)}, u32[]{:S(2)}) async-start(bf16[16,88,128]{2,1,0:T(8,128)(2,1)} %get-tuple-element.10), calls=%async_computation.1 | async-start | bytes 720896 | tf_op jit(solution)/shard_map/all_to_all | solution.py:245
  62.7 11.9 %collective-permute-start.4 = (bf16[4,160,128]{2,1,0:T(8,128)(2,1)S(1)}, bf16[4,160,128]{2,1,0:T(8,128)(2,1)S(1)}, u32[]{:S(2)}, u32[]{:S(2)}) collective-permute-start(bf16[4,160,128]{2,1,0:T(8,128)(2,1)S(1)} %pad_maximum_fusion), channel_id=1, source_target_pairs={{0,8},{8,0},{1,9},{9,1},{2,10},{10,2},{3,11},{11,3},{4,12},{12,4},... | collective-permute-start | bytes 491528 | tf_op jit(solution)/shard_map/ppermute | solution.py:250
  71.5 0.7 copy-start.2
  74.6 0.8 copy-start.5
  95.2 0.8 copy-start.4
  107.3 11.8 %all-to-all-start.2 = ((f32[16,40,128]{2,1,0:T(8,128)}), f32[16,40,128]{2,1,0:T(8,128)S(1)}, u32[]{:S(2)}, u32[]{:S(2)}) async-start(f32[16,40,128]{2,1,0:T(8,128)} %bitcast.17), calls=%async_computation.2 | async-start | bytes 655360 | tf_op jit(solution)/shard_map/all_to_all | solution.py:245
  119.1 0.7 copy-start.3

commit v4 on v3

--- a/solution.py
+++ b/solution.py
@@ -10,9 +10,9 @@
 from jax.sharding import PartitionSpec as P
 
 FINE = ("zh", "zl", "xl", "core", "xh", "y")
-COLS = ("xh", "xl", "y")
+COLS = ("zl", "xh", "xl")
 FAR = "zh"
-NEAR = "zl"
+NEAR = "y"
 
 LANES = 128
 ONES = 96
@@ -31,6 +31,10 @@
 
 VMEM = pl.BlockSpec(memory_space=pltpu.VMEM)
 SMEM = pl.BlockSpec(memory_space=pltpu.SMEM)
+
+
+def hold(value):
+    return pltpu.with_memory_space_constraint(value, pltpu.VMEM)
 
 
 def split3(value):
@@ -78,8 +82,8 @@
     return pl.pallas_call(
         pack_kernel,
         out_shape=(
-            jax.ShapeDtypeStruct((count, LANES), jnp.bfloat16),
-            jax.ShapeDtypeStruct((n_cols, count // 2 + 2 * GROUPS, LANES), jnp.bfloat16),
+            pltpu.VMEM((count, LANES), jnp.bfloat16),
+            pltpu.VMEM((n_cols, count // 2 + 2 * GROUPS, LANES), jnp.bfloat16),
         ),
         in_specs=[SMEM, VMEM, VMEM, VMEM, VMEM],
         out_specs=(VMEM, VMEM),
@@ -138,8 +142,8 @@
     return pl.pallas_call(
         weigh_kernel,
         out_shape=(
-            jax.ShapeDtypeStruct((2 * LANES, total), jnp.bfloat16),
-            jax.ShapeDtypeStruct((coregion.shape[0], total), jnp.float32),
+            pltpu.VMEM((2 * LANES, total), jnp.bfloat16),
+            pltpu.VMEM((coregion.shape[0], total), jnp.float32),
         ),
         in_specs=[VMEM, SMEM],
         out_specs=(VMEM, VMEM),
@@ -148,7 +152,7 @@
             pltpu.VMEM((1, total), jnp.float32),
         ],
         name="weigh",
-    )(cols, coregion)
+    )(hold(cols), coregion)
 
 
 def shaped(scaled_squared):
@@ -159,7 +163,8 @@
 
 
 def tile_kernel(n_sources, skip_own, unroll, own, *refs):
-    sources, (weights, factors, given, out, held, spread, sums) = refs[:n_sources], refs[n_sources:]
+    sources, (weights, factors), given = refs[:n_sources], refs[n_sources : n_sources + 2], refs[n_sources + 2 : -4]
+    out, held, spread, sums = refs[-4:]
     n_cols = weights.shape[1]
     n_tasks = factors.shape[0]
     n_rhs = LANES // n_tasks
@@ -205,27 +210,53 @@
                 * sums[task * n_rhs : (task + 1) * n_rhs, at : at + wide]
             )
         stacked.append(total)
-    out[...] = jnp.concatenate(stacked, axis=0).T + given[...]
-
-
-def tile(sources, own, weights, factors, given, skip_own, unroll):
+    result = jnp.concatenate(stacked, axis=0).T
+    for before in given:
+        result = result + before[...]
+    out[...] = result.astype(out.dtype)
+
+
+def tile(sources, own, weights, factors, given, skip_own, unroll, out_dtype=jnp.float32):
     n_cols = weights.shape[1]
     n_rows = sum((s.shape[0] - (1 if skip_own else 0)) * s.shape[1] for s in sources)
     return pl.pallas_call(
         functools.partial(tile_kernel, len(sources), skip_own, unroll),
-        out_shape=jax.ShapeDtypeStruct((n_cols // GROUPS, LANES), jnp.float32),
-        in_specs=[SMEM] + [VMEM] * (len(sources) + 3),
+        out_shape=pltpu.VMEM((n_cols // GROUPS, LANES), out_dtype),
+        in_specs=[SMEM] + [VMEM] * (len(sources) + 2 + len(given)),
         out_specs=VMEM,
         scratch_shapes=[
             pltpu.VMEM((n_rows, LANES), jnp.bfloat16),
             pltpu.VMEM((LANES, n_rows), jnp.bfloat16),
             pltpu.VMEM((LANES, n_cols), jnp.float32),
         ],
-    )(own, *sources, weights, factors, given)
+    )(own, *[hold(v) for v in sources], hold(weights), hold(factors), *[hold(v) for v in given])
+
+
+def join_kernel(*refs):
+    pieces, rows, copies = refs[:-2], refs[-2], refs[-1]
+    for index, piece in enumerate(pieces):
+        rows[index] = piece[...]
+        count = piece.shape[0]
+        for copy in range(copies.shape[0]):
+            copies[copy, index * count : (index + 1) * count] = piece[...]
+
+
+def join(pieces, n_copies):
+    count = pieces[0].shape[0]
+    return pl.pallas_call(
+        join_kernel,
+        out_shape=(
+            pltpu.VMEM((len(pieces), count, LANES), jnp.bfloat16),
+            pltpu.VMEM((n_copies, len(pieces) * count, LANES), jnp.bfloat16),
+        ),
+        in_specs=[VMEM] * len(pieces),
+        out_specs=(VMEM, VMEM),
+        name="join",
+    )(*[hold(piece) for piece in pieces])
 
 
 def finish_kernel(parts, rhs, noise, out):
-    total = jnp.sum(parts[...], axis=0).T
+    total = jnp.sum(parts[...].astype(jnp.float32), axis=0).T
     n_rhs, _ = rhs.shape
     groups = [total[index * n_rhs : (index + 1) * n_rhs] for index in range(GROUPS)]
     out[...] = jnp.concatenate(groups, axis=1) + noise[0] * rhs[...].astype(jnp.float32)
@@ -238,7 +269,7 @@
         in_specs=[VMEM, VMEM, SMEM],
         out_specs=VMEM,
         name="finish",
-    )(parts, rhs, noise)
+    )(hold(parts), rhs, noise)
 
 
 def exchange(blocks, axes):
@@ -257,17 +288,15 @@
     own_rows, own_cols = pack(at, points.T, rhs.T, task_ids, length_scales, across)
     others = [from_shift(own_rows, FAR, shift) for shift in (far // 2, 1, far - 1)]
     cols = exchange(own_cols, COLS)
-    rows = jnp.stack([own_rows] + others)
+    rows, copies = join([own_rows] + others, near)
     twin = from_shift(rows, "core", 1)
-    rows = rows.reshape(1, -1, LANES)
-    all_rows = exchange(jnp.broadcast_to(rows, (near,) + rows.shape[1:]), NEAR)
+    all_rows = exchange(copies, NEAR)
     weights, factors = weigh(cols, coregion)
-    empty = jnp.zeros((weights.shape[1] // GROUPS, LANES), jnp.float32)
-    first = (rows, twin.reshape(rows.shape))
-    total = tile(first, own, weights, factors, empty, False, 5)
+    first = [value.reshape(1, -1, LANES) for value in (rows, twin)]
+    total = tile(first, own, weights, factors, [], False, 10)
     twins = from_shift(all_rows, "core", 1)
-    total = tile((all_rows,), own, weights, factors, total, True, 2)
-    total = tile((twins,), own, weights, factors, total, True, 2)
+    total = tile([all_rows], own, weights, factors, [total], True, 10)
+    total = tile([twins], own, weights, factors, [total], True, 10, jnp.bfloat16)
     back = exchange(total.reshape(across, -1, LANES), COLS)
     return finish(back, rhs.T, noise).T
 

time: 122 us -> 108 us (0.89)
  the two profiles are of different devices: /device:TPU:1 before, /device:TPU:2 now
where the time goes in v4:
time: 108 us; the launch traced here: 107 us
  starting transfers between devices  42.3 us (39%)
  Pallas kernels  29.6 us (27%)
  waiting for transfers between devices  16.6 us (15%)
  blocking collectives  13.5 us (12%)
  local copies, waits for them, and re-layouts  4.1 us (4%)
    ppermute x5, starting transfers between devices, from_shift(): lax.ppermute(value, axis, [(i, (i + shift) % count) for i in range(count)])  29.8 us
    pallas_call x3, Pallas kernels, tile(): pl.pallas_call(functools.partial(tile_kernel, len(sources), skip_own, unr...  25.1 us
    all_to_all x1, blocking collectives, exchange(): return lax.all_to_all(blocks, axes, 0, 0, tiled=True)  13.5 us
    all_to_all x2, starting transfers between devices, exchange(): return lax.all_to_all(blocks, axes, 0, 0, tiled=True)  12.5 us
    all_to_all x2, waiting for transfers between devices, exchange(): return lax.all_to_all(blocks, axes, 0, 0, tiled=True)  12.3 us
    ppermute x5, waiting for transfers between devices, from_shift(): lax.ppermute(value, axis, [(i, (i + shift) % count) for i in range(count)])  4.34 us
    unnamed x8, local copies, waits for them, and re-layouts  4.1 us
  transfers between devices with their start and end apart: 7, of which 4 were waited for; matrix products, arithmetic and copies ran while one was open for 0% of the time, Pallas kernels for 15%

profile of v4, /device:TPU:2, one launch (start us, length us, event | category | flops | bytes accessed | tf_op | source)
XLA Modules:
  0.0 106.8 jit_solution(14379052337315821476)
XLA Ops:
  0.0 1.8 %pack.1 = (bf16[160,128]{1,0:T(8,128)(2,1)S(1)}, bf16[16,88,128]{2,1,0:T(8,128)(2,1)}) custom-call(s32[1]{0:T(128)} %bitcast.1.at_ref, bf16[64,160]{1,0:T(8,128)(2,1)} %bitcast.14, bf16[32,160]{1,0:T(8,128)(2,1)} %bitcast.12, s32[1,160]{1,0:T(1,128)} %bitcast.15, f32[1,64]{1,0:T(1,128)} %bitcast.16), custom_call_target="tpu_custom_call" | custom-call | tf_op jit(solution)/shard_map/pack/pallas_call | solution.py:82
  1.9 15.7 %collective-permute-start = (bf16[160,128]{1,0:T(8,128)(2,1)S(1)}, bf16[160,128]{1,0:T(8,128)(2,1)S(1)}, u32[]{:S(2)}, u32[]{:S(2)}) collective-permute-start(bf16[160,128]{1,0:T(8,128)(2,1)S(1)} %get-tuple-element.11.refs_0_), channel_id=1, source_target_pairs={{0,256},{128,384},{256,0},{384,128},{1,257},{129,385},{257,1},{385... | collective-permute-start | bytes 122888 | tf_op jit(solution)/shard_map/ppermute | solution.py:281
  17.6 4.3 %collective-permute-start.1 = (bf16[160,128]{1,0:T(8,128)(2,1)S(1)}, bf16[160,128]{1,0:T(8,128)(2,1)S(1)}, u32[]{:S(2)}, u32[]{:S(2)}) collective-permute-start(bf16[160,128]{1,0:T(8,128)(2,1)S(1)} %get-tuple-element.11.refs_0_), channel_id=1, source_target_pairs={{0,128},{128,256},{256,384},{384,0},{1,129},{129,257},{257,385},{3... | collective-permute-start | bytes 122888 | tf_op jit(solution)/shard_map/ppermute | solution.py:281
  21.9 5.5 %collective-permute-start.2 = (bf16[160,128]{1,0:T(8,128)(2,1)S(1)}, bf16[160,128]{1,0:T(8,128)(2,1)S(1)}, u32[]{:S(2)}, u32[]{:S(2)}) collective-permute-start(bf16[160,128]{1,0:T(8,128)(2,1)S(1)} %get-tuple-element.11.refs_0_), channel_id=1, source_target_pairs={{0,384},{128,0},{256,128},{384,256},{1,385},{129,1},{257,129},{385... | collective-permute-start | bytes 122888 | tf_op jit(solution)/shard_map/ppermute | solution.py:281
  27.3 0.0 collective-permute-done.refs_1_
  27.3 1.8 %collective-permute-done.1.refs_2_ = bf16[160,128]{1,0:T(8,128)(2,1)S(1)} collective-permute-done((bf16[160,128]{1,0:T(8,128)(2,1)S(1)}, bf16[160,128]{1,0:T(8,128)(2,1)S(1)}, u32[]{:S(2)}, u32[]{:S(2)}) %collective-permute-start.1) | collective-permute-done | bytes 40992 | tf_op jit(solution)/shard_map/ppermute | solution.py:281
  29.1 2.6 %collective-permute-done.2.refs_3_ = bf16[160,128]{1,0:T(8,128)(2,1)S(1)} collective-permute-done((bf16[160,128]{1,0:T(8,128)(2,1)S(1)}, bf16[160,128]{1,0:T(8,128)(2,1)S(1)}, u32[]{:S(2)}, u32[]{:S(2)}) %collective-permute-start.2) | collective-permute-done | bytes 40992 | tf_op jit(solution)/shard_map/ppermute | solution.py:281
  31.7 0.1 join.1
  31.8 13.5 %all_to_all.15.refs_0_ = bf16[4,640,128]{2,1,0:T(8,128)(2,1)} all-to-all(bf16[4,640,128]{2,1,0:T(8,128)(2,1)S(1)} %get-tuple-element.12), channel_id=1, replica_groups=mesh['zh'=4,'zl'=4,'xl'=2,'core'=2,'xh'=2,'y'=4] {'y'}, dimensions={0} | all-to-all | bytes 1310720 | tf_op jit(solution)/shard_map/all_to_all | solution.py:276
  45.3 7.4 %all-to-all-start.1 = ((bf16[16,88,128]{2,1,0:T(8,128)(2,1)}), bf16[16,88,128]{2,1,0:T(8,128)(2,1)S(1)}, u32[]{:S(2)}, u32[]{:S(2)}) async-start(bf16[16,88,128]{2,1,0:T(8,128)(2,1)} %get-tuple-element.13), calls=%async_computation.1 | async-start | bytes 720896 | tf_op jit(solution)/shard_map/all_to_all | solution.py:276
  52.7 1.9 %collective-permute-start.3 = (bf16[4,640,128]{2,1,0:T(8,128)(2,1)}, bf16[4,640,128]{2,1,0:T(8,128)(2,1)}, u32[]{:S(2)}, u32[]{:S(2)}) collective-permute-start(bf16[4,640,128]{2,1,0:T(8,128)(2,1)} %all_to_all.15.refs_0_), channel_id=1, source_target_pairs={{0,8},{8,0},{1,9},{9,1},{2,10},{10,2},{3,11},{11,3},{4,12},{12,4},... | collective-permute-start | bytes 1966088 | tf_op jit(solution)/shard_map/ppermute | solution.py:281
  54.6 2.4 %collective-permute-start.4 = (bf16[4,160,128]{2,1,0:T(8,128)(2,1)S(1)}, bf16[4,160,128]{2,1,0:T(8,128)(2,1)S(1)}, u32[]{:S(2)}, u32[]{:S(2)}) collective-permute-start(bf16[4,160,128]{2,1,0:T(8,128)(2,1)S(1)} %get-tuple-element.16), channel_id=1, source_target_pairs={{0,8},{8,0},{1,9},{9,1},{2,10},{10,2},{3,11},{11,3},{4,12},{12,4},... | collective-permute-start | bytes 491528 | tf_op jit(solution)/shard_map/ppermute | solution.py:281
  57.0 5.1 %all-to-all-done.1.cols = bf16[16,88,128]{2,1,0:T(8,128)(2,1)S(1)} async-done(((bf16[16,88,128]{2,1,0:T(8,128)(2,1)}), bf16[16,88,128]{2,1,0:T(8,128)(2,1)S(1)}, u32[]{:S(2)}, u32[]{:S(2)}) %all-to-all-start.1) | async-done | bytes 360480 | tf_op jit(solution)/shard_map/all_to_all | solution.py:276
  62.1 1.0 weigh.1
  63.1 0.0 collective-permute-done.4
  63.2 6.0 %shard_map.64.refs_3_ = f32[640,128]{1,0:T(8,128)S(1)} custom-call(s32[1]{0:T(128)} %bitcast.own, bf16[1,640,128]{2,1,0:T(8,128)(2,1)S(1)} %bitcast.10, bf16[1,640,128]{2,1,0:T(8,128)(2,1)S(1)} %bitcast.11, bf16[256,2560]{1,0:T(8,128)(2,1)S(1)} %get-tuple-element.14.refs_2_.refs_1_, f32[4,2560]{1,0:T(4,128)S(1)} %get-tuple-element.15.refs_3_.refs_2_), custom_call_target="tpu_custom_call" | custom-call | tf_op jit(solution)/shard_map/pallas_call | solution.py:222
  69.2 0.0 copy-start
  69.2 1.1 copy-done
  70.3 0.0 copy-start.2
  70.3 0.8 copy-done.2
  71.0 0.0 copy-start.1
  71.0 1.3 %copy-done.1 = bf16[256,2560]{1,0:T(8,128)(2,1)S(1)} copy-done((bf16[256,2560]{1,0:T(8,128)(2,1)S(1)}, bf16[256,2560]{1,0:T(8,128)(2,1)}, u32[]{:S(2)}) %copy-start.1) | copy-done | bytes 1310744
  72.3 0.0 copy-start.3
  72.3 1.0 copy-done.3
  73.3 9.3 %shard_map.65.refs_3_ = f32[640,128]{1,0:T(8,128)S(1)} custom-call(s32[1]{0:T(128)} %bitcast.own, bf16[4,640,128]{2,1,0:T(8,128)(2,1)} %all_to_all.15.refs_0_, bf16[256,2560]{1,0:T(8,128)(2,1)S(1)} %copy-done.1, f32[4,2560]{1,0:T(4,128)S(1)} %get-tuple-element.15.refs_3_.refs_2_, f32[640,128]{1,0:T(8,128)S(1)} %copy-done.3), custom_call_target="tpu_custom_call" | custom-call | tf_op jit(solution)/shard_map/pallas_call | solution.py:222
  82.6 0.0 collective-permute-done.3.refs_0_
  82.6 9.8 %shard_map.66 = bf16[640,128]{1,0:T(8,128)(2,1)} custom-call(s32[1]{0:T(128)} %bitcast.own, bf16[4,640,128]{2,1,0:T(8,128)(2,1)} %collective-permute-done.3.refs_0_, bf16[256,2560]{1,0:T(8,128)(2,1)S(1)} %copy-done.1, f32[4,2560]{1,0:T(4,128)S(1)} %get-tuple-element.15.refs_3_.refs_2_, f32[640,128]{1,0:T(8,128)S(1)} %shard_map.65.refs_3_), custom_call_target="tpu_custom_call" | custom-call | tf_op jit(solution)/shard_map/pallas_call | solution.py:222
  92.4 5.1 %all-to-all-start.2 = ((bf16[16,40,128]{2,1,0:T(8,128)(2,1)}), bf16[16,40,128]{2,1,0:T(8,128)(2,1)S(1)}, u32[]{:S(2)}, u32[]{:S(2)}) async-start(bf16[16,40,128]{2,1,0:T(8,128)(2,1)} %bitcast.8), calls=%async_computation.2 | async-start | bytes 327680 | tf_op jit(solution)/shard_map/all_to_all | solution.py:276
  98.1 7.2 %all-to-all-done.2.parts = bf16[16,40,128]{2,1,0:T(8,128)(2,1)S(1)} async-done(((bf16[16,40,128]{2,1,0:T(8,128)(2,1)}), bf16[16,40,128]{2,1,0:T(8,128)(2,1)S(1)}, u32[]{:S(2)}, u32[]{:S(2)}) %all-to-all-start.2) | async-done | bytes 163872 | tf_op jit(solution)/shard_map/all_to_all | solution.py:276
  105.3 1.5 %finish.1 = f32[32,160]{1,0:T(8,128)} custom-call(bf16[16,40,128]{2,1,0:T(8,128)(2,1)S(1)} %all-to-all-done.2.parts, bf16[32,160]{1,0:T(8,128)(2,1)} %bitcast.13, f32[1]{0:T(128)S(6)} %copy.7.noise), custom_call_target="tpu_custom_call" | custom-call | tf_op jit(solution)/shard_map/finish/pallas_call | solution.py:266
Async XLA Ops:
  1.9 25.5 %collective-permute-start = (bf16[160,128]{1,0:T(8,128)(2,1)S(1)}, bf16[160,128]{1,0:T(8,128)(2,1)S(1)}, u32[]{:S(2)}, u32[]{:S(2)}) collective-permute-start(bf16[160,128]{1,0:T(8,128)(2,1)S(1)} %get-tuple-element.11.refs_0_), channel_id=1, source_target_pairs={{0,256},{128,384},{256,0},{384,128},{1,257},{129,385},{257,1},{385... | collective-permute-start | bytes 122888 | tf_op jit(solution)/shard_map/ppermute | solution.py:281
  17.6 11.5 %collective-permute-start.1 = (bf16[160,128]{1,0:T(8,128)(2,1)S(1)}, bf16[160,128]{1,0:T(8,128)(2,1)S(1)}, u32[]{:S(2)}, u32[]{:S(2)}) collective-permute-start(bf16[160,128]{1,0:T(8,128)(2,1)S(1)} %get-tuple-element.11.refs_0_), channel_id=1, source_target_pairs={{0,128},{128,256},{256,384},{384,0},{1,129},{129,257},{257,385},{3... | collective-permute-start | bytes 122888 | tf_op jit(solution)/shard_map/ppermute | solution.py:281
  21.9 9.8 %collective-permute-start.2 = (bf16[160,128]{1,0:T(8,128)(2,1)S(1)}, bf16[160,128]{1,0:T(8,128)(2,1)S(1)}, u32[]{:S(2)}, u32[]{:S(2)}) collective-permute-start(bf16[160,128]{1,0:T(8,128)(2,1)S(1)} %get-tuple-element.11.refs_0_), channel_id=1, source_target_pairs={{0,384},{128,0},{256,128},{384,256},{1,385},{129,1},{257,129},{385... | collective-permute-start | bytes 122888 | tf_op jit(solution)/shard_map/ppermute | solution.py:281
  45.3 16.8 %all-to-all-start.1 = ((bf16[16,88,128]{2,1,0:T(8,128)(2,1)}), bf16[16,88,128]{2,1,0:T(8,128)(2,1)S(1)}, u32[]{:S(2)}, u32[]{:S(2)}) async-start(bf16[16,88,128]{2,1,0:T(8,128)(2,1)} %get-tuple-element.13), calls=%async_computation.1 | async-start | bytes 720896 | tf_op jit(solution)/shard_map/all_to_all | solution.py:276
  52.7 29.9 %collective-permute-start.3 = (bf16[4,640,128]{2,1,0:T(8,128)(2,1)}, bf16[4,640,128]{2,1,0:T(8,128)(2,1)}, u32[]{:S(2)}, u32[]{:S(2)}) collective-permute-start(bf16[4,640,128]{2,1,0:T(8,128)(2,1)} %all_to_all.15.refs_0_), channel_id=1, source_target_pairs={{0,8},{8,0},{1,9},{9,1},{2,10},{10,2},{3,11},{11,3},{4,12},{12,4},... | collective-permute-start | bytes 1966088 | tf_op jit(solution)/shard_map/ppermute | solution.py:281
  54.6 8.5 %collective-permute-start.4 = (bf16[4,160,128]{2,1,0:T(8,128)(2,1)S(1)}, bf16[4,160,128]{2,1,0:T(8,128)(2,1)S(1)}, u32[]{:S(2)}, u32[]{:S(2)}) collective-permute-start(bf16[4,160,128]{2,1,0:T(8,128)(2,1)S(1)} %get-tuple-element.16), channel_id=1, source_target_pairs={{0,8},{8,0},{1,9},{9,1},{2,10},{10,2},{3,11},{11,3},{4,12},{12,4},... | collective-permute-start | bytes 491528 | tf_op jit(solution)/shard_map/ppermute | solution.py:281
  69.2 1.1 %copy-start = (bf16[256,2560]{1,0:T(8,128)(2,1)}, bf16[256,2560]{1,0:T(8,128)(2,1)S(1)}, u32[]{:S(2)}) copy-start(bf16[256,2560]{1,0:T(8,128)(2,1)S(1)} %get-tuple-element.14.refs_2_.refs_1_) | copy-start | bytes 3932164
  70.3 0.8 copy-start.2
  71.0 1.3 %copy-start.1 = (bf16[256,2560]{1,0:T(8,128)(2,1)S(1)}, bf16[256,2560]{1,0:T(8,128)(2,1)}, u32[]{:S(2)}) copy-start(bf16[256,2560]{1,0:T(8,128)(2,1)} %copy-done) | copy-start | bytes 3932164
  72.3 1.0 copy-start.3
  92.4 12.9 %all-to-all-start.2 = ((bf16[16,40,128]{2,1,0:T(8,128)(2,1)}), bf16[16,40,128]{2,1,0:T(8,128)(2,1)S(1)}, u32[]{:S(2)}, u32[]{:S(2)}) async-start(bf16[16,40,128]{2,1,0:T(8,128)(2,1)} %bitcast.8), calls=%async_computation.2 | async-start | bytes 327680 | tf_op jit(solution)/shard_map/all_to_all | solution.py:276

commit v5 on v4

--- a/solution.py
+++ b/solution.py
@@ -30,6 +30,7 @@
 
 
 VMEM = pl.BlockSpec(memory_space=pltpu.VMEM)
+ANY = pl.BlockSpec(memory_space=pl.ANY)
 SMEM = pl.BlockSpec(memory_space=pltpu.SMEM)
 
 
@@ -163,19 +164,26 @@
 
 
 def tile_kernel(n_sources, skip_own, unroll, own, *refs):
-    sources, (weights, factors), given = refs[:n_sources], refs[n_sources : n_sources + 2], refs[n_sources + 2 : -4]
-    out, held, spread, sums = refs[-4:]
+    sources, (weights, factors), given = refs[:n_sources], refs[n_sources : n_sources + 2], refs[n_sources + 2 : -5]
+    out, held, spread, sums, arrived = refs[-5:]
     n_cols = weights.shape[1]
     n_tasks = factors.shape[0]
     n_rhs = LANES // n_tasks
 
-    at = 0
+    at, copies = 0, []
     for source in sources:
         blocks, count, _ = source.shape
         for index in range(1, blocks) if skip_own else range(blocks):
             place = lax.rem(own[0] + index, blocks) if skip_own else index
-            held[at : at + count] = source[place]
+            target = held.at[pl.ds(at, count)]
+            copies.append(
+                pltpu.make_async_copy(source.at[place], target, arrived.at[len(copies)])
+            )
             at += count
+    for copy in copies:
+        copy.start()
+    for copy in copies:
+        copy.wait()
 
     turned = held[...].astype(jnp.float32).T
     vectors = turned[64 : 64 + n_rhs, :]
@@ -222,14 +230,15 @@
     return pl.pallas_call(
         functools.partial(tile_kernel, len(sources), skip_own, unroll),
         out_shape=pltpu.VMEM((n_cols // GROUPS, LANES), out_dtype),
-        in_specs=[SMEM] + [VMEM] * (len(sources) + 2 + len(given)),
+        in_specs=[SMEM] + [ANY] * len(sources) + [VMEM] * (2 + len(given)),
         out_specs=VMEM,
         scratch_shapes=[
             pltpu.VMEM((n_rows, LANES), jnp.bfloat16),
             pltpu.VMEM((LANES, n_rows), jnp.bfloat16),
             pltpu.VMEM((LANES, n_cols), jnp.float32),
+            pltpu.SemaphoreType.DMA((4,)),
         ],
-    )(own, *[hold(v) for v in sources], hold(weights), hold(factors), *[hold(v) for v in given])
+    )(own, *(sources if skip_own else [hold(v) for v in sources]), hold(weights), hold(factors), *[hold(v) for v in given])
 
 
 def join_kernel(*refs):

time: 108 us -> 104 us (0.963)
  local copies, waits for them, and re-layouts: 4.1 us -> 0 us
    unnamed x8 -> x0, local copies, waits for them, and re-layouts: 4.1 us -> none
  transfers between devices with their start and end apart: 7 -> 7, of which waited for: 4 -> 4; matrix products, arithmetic and copies ran while one was open for 0% -> 0% of each run, Pallas kernels for 15% -> 16%
where the time goes in v5:
time: 104 us; the launch traced here: 103 us
  starting transfers between devices  42.3 us (41%)
  Pallas kernels  30.1 us (29%)
  waiting for transfers between devices  16.6 us (16%)
  blocking collectives  13.5 us (13%)
    ppermute x5, starting transfers between devices, from_shift(): lax.ppermute(value, axis, [(i, (i + shift) % count) for i in range(count)])  29.8 us
    pallas_call x3, Pallas kernels, tile(): pl.pallas_call(functools.partial(tile_kernel, len(sources), skip_own, unr...  25.5 us
    all_to_all x1, blocking collectives, exchange(): return lax.all_to_all(blocks, axes, 0, 0, tiled=True)  13.5 us
    all_to_all x2, starting transfers between devices, exchange(): return lax.all_to_all(blocks, axes, 0, 0, tiled=True)  12.5 us
    all_to_all x2, waiting for transfers between devices, exchange(): return lax.all_to_all(blocks, axes, 0, 0, tiled=True)  12.3 us
    ppermute x5, waiting for transfers between devices, from_shift(): lax.ppermute(value, axis, [(i, (i + shift) % count) for i in range(count)])  4.34 us
  transfers between devices with their start and end apart: 7, of which 4 were waited for; matrix products, arithmetic and copies ran while one was open for 0% of the time, Pallas kernels for 16%

profile of v5, /device:TPU:2, one launch (start us, length us, event | category | flops | bytes accessed | tf_op | source)
XLA Modules:
  0.0 103.2 jit_solution(2069493293306241082)
XLA Ops:
  0.0 1.9 %pack.1 = (bf16[160,128]{1,0:T(8,128)(2,1)S(1)}, bf16[16,88,128]{2,1,0:T(8,128)(2,1)}) custom-call(s32[1]{0:T(128)} %bitcast.1.at_ref, bf16[64,160]{1,0:T(8,128)(2,1)} %bitcast.14, bf16[32,160]{1,0:T(8,128)(2,1)} %bitcast.12, s32[1,160]{1,0:T(1,128)} %bitcast.15, f32[1,64]{1,0:T(1,128)} %bitcast.16), custom_call_target="tpu_custom_call" | custom-call | tf_op jit(solution)/shard_map/pack/pallas_call | solution.py:83
  1.9 15.7 %collective-permute-start = (bf16[160,128]{1,0:T(8,128)(2,1)S(1)}, bf16[160,128]{1,0:T(8,128)(2,1)S(1)}, u32[]{:S(2)}, u32[]{:S(2)}) collective-permute-start(bf16[160,128]{1,0:T(8,128)(2,1)S(1)} %get-tuple-element.11.refs_0_), channel_id=1, source_target_pairs={{0,256},{128,384},{256,0},{384,128},{1,257},{129,385},{257,1},{385... | collective-permute-start | bytes 122888 | tf_op jit(solution)/shard_map/ppermute | solution.py:290
  17.6 4.3 %collective-permute-start.1 = (bf16[160,128]{1,0:T(8,128)(2,1)S(1)}, bf16[160,128]{1,0:T(8,128)(2,1)S(1)}, u32[]{:S(2)}, u32[]{:S(2)}) collective-permute-start(bf16[160,128]{1,0:T(8,128)(2,1)S(1)} %get-tuple-element.11.refs_0_), channel_id=1, source_target_pairs={{0,128},{128,256},{256,384},{384,0},{1,129},{129,257},{257,385},{3... | collective-permute-start | bytes 122888 | tf_op jit(solution)/shard_map/ppermute | solution.py:290
  21.9 5.5 %collective-permute-start.2 = (bf16[160,128]{1,0:T(8,128)(2,1)S(1)}, bf16[160,128]{1,0:T(8,128)(2,1)S(1)}, u32[]{:S(2)}, u32[]{:S(2)}) collective-permute-start(bf16[160,128]{1,0:T(8,128)(2,1)S(1)} %get-tuple-element.11.refs_0_), channel_id=1, source_target_pairs={{0,384},{128,0},{256,128},{384,256},{1,385},{129,1},{257,129},{385... | collective-permute-start | bytes 122888 | tf_op jit(solution)/shard_map/ppermute | solution.py:290
  27.3 0.0 collective-permute-done.refs_1_
  27.3 1.8 %collective-permute-done.1.refs_2_ = bf16[160,128]{1,0:T(8,128)(2,1)S(1)} collective-permute-done((bf16[160,128]{1,0:T(8,128)(2,1)S(1)}, bf16[160,128]{1,0:T(8,128)(2,1)S(1)}, u32[]{:S(2)}, u32[]{:S(2)}) %collective-permute-start.1) | collective-permute-done | bytes 40992 | tf_op jit(solution)/shard_map/ppermute | solution.py:290
  29.1 2.6 %collective-permute-done.2.refs_3_ = bf16[160,128]{1,0:T(8,128)(2,1)S(1)} collective-permute-done((bf16[160,128]{1,0:T(8,128)(2,1)S(1)}, bf16[160,128]{1,0:T(8,128)(2,1)S(1)}, u32[]{:S(2)}, u32[]{:S(2)}) %collective-permute-start.2) | collective-permute-done | bytes 40992 | tf_op jit(solution)/shard_map/ppermute | solution.py:290
  31.7 0.1 join.1
  31.8 13.5 %all_to_all.15.refs_0_ = bf16[4,640,128]{2,1,0:T(8,128)(2,1)} all-to-all(bf16[4,640,128]{2,1,0:T(8,128)(2,1)S(1)} %get-tuple-element.12), channel_id=1, replica_groups=mesh['zh'=4,'zl'=4,'xl'=2,'core'=2,'xh'=2,'y'=4] {'y'}, dimensions={0} | all-to-all | bytes 1310720 | tf_op jit(solution)/shard_map/all_to_all | solution.py:285
  45.3 7.4 %all-to-all-start.1 = ((bf16[16,88,128]{2,1,0:T(8,128)(2,1)}), bf16[16,88,128]{2,1,0:T(8,128)(2,1)S(1)}, u32[]{:S(2)}, u32[]{:S(2)}) async-start(bf16[16,88,128]{2,1,0:T(8,128)(2,1)} %get-tuple-element.13), calls=%async_computation.1 | async-start | bytes 720896 | tf_op jit(solution)/shard_map/all_to_all | solution.py:285
  52.7 1.9 %collective-permute-start.3 = (bf16[4,640,128]{2,1,0:T(8,128)(2,1)}, bf16[4,640,128]{2,1,0:T(8,128)(2,1)}, u32[]{:S(2)}, u32[]{:S(2)}) collective-permute-start(bf16[4,640,128]{2,1,0:T(8,128)(2,1)} %all_to_all.15.refs_0_), channel_id=1, source_target_pairs={{0,8},{8,0},{1,9},{9,1},{2,10},{10,2},{3,11},{11,3},{4,12},{12,4},... | collective-permute-start | bytes 1966088 | tf_op jit(solution)/shard_map/ppermute | solution.py:290
  54.6 2.4 %collective-permute-start.4 = (bf16[4,160,128]{2,1,0:T(8,128)(2,1)S(1)}, bf16[4,160,128]{2,1,0:T(8,128)(2,1)S(1)}, u32[]{:S(2)}, u32[]{:S(2)}) collective-permute-start(bf16[4,160,128]{2,1,0:T(8,128)(2,1)S(1)} %get-tuple-element.16), channel_id=1, source_target_pairs={{0,8},{8,0},{1,9},{9,1},{2,10},{10,2},{3,11},{11,3},{4,12},{12,4},... | collective-permute-start | bytes 491528 | tf_op jit(solution)/shard_map/ppermute | solution.py:290
  57.0 5.1 %all-to-all-done.1.cols = bf16[16,88,128]{2,1,0:T(8,128)(2,1)S(1)} async-done(((bf16[16,88,128]{2,1,0:T(8,128)(2,1)}), bf16[16,88,128]{2,1,0:T(8,128)(2,1)S(1)}, u32[]{:S(2)}, u32[]{:S(2)}) %all-to-all-start.1) | async-done | bytes 360480 | tf_op jit(solution)/shard_map/all_to_all | solution.py:285
  62.1 1.0 %weigh.1 = (bf16[256,2560]{1,0:T(8,128)(2,1)S(1)}, f32[4,2560]{1,0:T(4,128)S(1)}) custom-call(bf16[16,88,128]{2,1,0:T(8,128)(2,1)S(1)} %all-to-all-done.1.cols, f32[4,4]{1,0:T(4,128)} %coregion.1), custom_call_target="tpu_custom_call" | custom-call | tf_op jit(solution)/shard_map/weigh/pallas_call | solution.py:143
  63.2 0.0 collective-permute-done.4
  63.2 6.5 %shard_map.64.refs_3_ = f32[640,128]{1,0:T(8,128)S(1)} custom-call(s32[1]{0:T(128)} %bitcast.own, bf16[1,640,128]{2,1,0:T(8,128)(2,1)S(1)} %bitcast.10, bf16[1,640,128]{2,1,0:T(8,128)(2,1)S(1)} %bitcast.11, bf16[256,2560]{1,0:T(8,128)(2,1)S(1)} %get-tuple-element.14.refs_2_.refs_1_, f32[4,2560]{1,0:T(4,128)S(1)} %get-tuple-element.15.refs_3_.refs_2_), custom_call_target="tpu_custom_call" | custom-call | tf_op jit(solution)/shard_map/pallas_call | solution.py:230
  69.6 9.3 %shard_map.65.refs_3_ = f32[640,128]{1,0:T(8,128)S(1)} custom-call(s32[1]{0:T(128)} %bitcast.own, bf16[4,640,128]{2,1,0:T(8,128)(2,1)} %all_to_all.15.refs_0_, bf16[256,2560]{1,0:T(8,128)(2,1)S(1)} %get-tuple-element.14.refs_2_.refs_1_, f32[4,2560]{1,0:T(4,128)S(1)} %get-tuple-element.15.refs_3_.refs_2_, f32[640,128]{1,0:T(8,128)S(1)} %shard_map.64.refs_3_), custom_call_target="tpu_custom_call" | custom-call | tf_op jit(solution)/shard_map/pallas_call | solution.py:230
  78.9 0.0 collective-permute-done.3.refs_0_
  79.0 9.8 %shard_map.66 = bf16[640,128]{1,0:T(8,128)(2,1)} custom-call(s32[1]{0:T(128)} %bitcast.own, bf16[4,640,128]{2,1,0:T(8,128)(2,1)} %collective-permute-done.3.refs_0_, bf16[256,2560]{1,0:T(8,128)(2,1)S(1)} %get-tuple-element.14.refs_2_.refs_1_, f32[4,2560]{1,0:T(4,128)S(1)} %get-tuple-element.15.refs_3_.refs_2_, f32[640,128]{1,0:T(8,128)S(1)} %shard_map.65.refs_3_), custom_call_target="tpu_custom_call" | custom-call | tf_op jit(solution)/shard_map/pallas_call | solution.py:230
  88.7 5.1 %all-to-all-start.2 = ((bf16[16,40,128]{2,1,0:T(8,128)(2,1)}), bf16[16,40,128]{2,1,0:T(8,128)(2,1)S(1)}, u32[]{:S(2)}, u32[]{:S(2)}) async-start(bf16[16,40,128]{2,1,0:T(8,128)(2,1)} %bitcast.8), calls=%async_computation.2 | async-start | bytes 327680 | tf_op jit(solution)/shard_map/all_to_all | solution.py:285
  94.5 7.2 %all-to-all-done.2.parts = bf16[16,40,128]{2,1,0:T(8,128)(2,1)S(1)} async-done(((bf16[16,40,128]{2,1,0:T(8,128)(2,1)}), bf16[16,40,128]{2,1,0:T(8,128)(2,1)S(1)}, u32[]{:S(2)}, u32[]{:S(2)}) %all-to-all-start.2) | async-done | bytes 163872 | tf_op jit(solution)/shard_map/all_to_all | solution.py:285
  101.7 1.5 %finish.1 = f32[32,160]{1,0:T(8,128)} custom-call(bf16[16,40,128]{2,1,0:T(8,128)(2,1)S(1)} %all-to-all-done.2.parts, bf16[32,160]{1,0:T(8,128)(2,1)} %bitcast.13, f32[1]{0:T(128)S(6)} %copy.7.noise), custom_call_target="tpu_custom_call" | custom-call | tf_op jit(solution)/shard_map/finish/pallas_call | solution.py:275
Async XLA Ops:
  1.9 25.5 %collective-permute-start = (bf16[160,128]{1,0:T(8,128)(2,1)S(1)}, bf16[160,128]{1,0:T(8,128)(2,1)S(1)}, u32[]{:S(2)}, u32[]{:S(2)}) collective-permute-start(bf16[160,128]{1,0:T(8,128)(2,1)S(1)} %get-tuple-element.11.refs_0_), channel_id=1, source_target_pairs={{0,256},{128,384},{256,0},{384,128},{1,257},{129,385},{257,1},{385... | collective-permute-start | bytes 122888 | tf_op jit(solution)/shard_map/ppermute | solution.py:290
  17.6 11.5 %collective-permute-start.1 = (bf16[160,128]{1,0:T(8,128)(2,1)S(1)}, bf16[160,128]{1,0:T(8,128)(2,1)S(1)}, u32[]{:S(2)}, u32[]{:S(2)}) collective-permute-start(bf16[160,128]{1,0:T(8,128)(2,1)S(1)} %get-tuple-element.11.refs_0_), channel_id=1, source_target_pairs={{0,128},{128,256},{256,384},{384,0},{1,129},{129,257},{257,385},{3... | collective-permute-start | bytes 122888 | tf_op jit(solution)/shard_map/ppermute | solution.py:290
  21.9 9.8 %collective-permute-start.2 = (bf16[160,128]{1,0:T(8,128)(2,1)S(1)}, bf16[160,128]{1,0:T(8,128)(2,1)S(1)}, u32[]{:S(2)}, u32[]{:S(2)}) collective-permute-start(bf16[160,128]{1,0:T(8,128)(2,1)S(1)} %get-tuple-element.11.refs_0_), channel_id=1, source_target_pairs={{0,384},{128,0},{256,128},{384,256},{1,385},{129,1},{257,129},{385... | collective-permute-start | bytes 122888 | tf_op jit(solution)/shard_map/ppermute | solution.py:290
  45.3 16.8 %all-to-all-start.1 = ((bf16[16,88,128]{2,1,0:T(8,128)(2,1)}), bf16[16,88,128]{2,1,0:T(8,128)(2,1)S(1)}, u32[]{:S(2)}, u32[]{:S(2)}) async-start(bf16[16,88,128]{2,1,0:T(8,128)(2,1)} %get-tuple-element.13), calls=%async_computation.1 | async-start | bytes 720896 | tf_op jit(solution)/shard_map/all_to_all | solution.py:285
  52.7 26.2 %collective-permute-start.3 = (bf16[4,640,128]{2,1,0:T(8,128)(2,1)}, bf16[4,640,128]{2,1,0:T(8,128)(2,1)}, u32[]{:S(2)}, u32[]{:S(2)}) collective-permute-start(bf16[4,640,128]{2,1,0:T(8,128)(2,1)} %all_to_all.15.refs_0_), channel_id=1, source_target_pairs={{0,8},{8,0},{1,9},{9,1},{2,10},{10,2},{3,11},{11,3},{4,12},{12,4},... | collective-permute-start | bytes 1966088 | tf_op jit(solution)/shard_map/ppermute | solution.py:290
  54.6 8.5 %collective-permute-start.4 = (bf16[4,160,128]{2,1,0:T(8,128)(2,1)S(1)}, bf16[4,160,128]{2,1,0:T(8,128)(2,1)S(1)}, u32[]{:S(2)}, u32[]{:S(2)}) collective-permute-start(bf16[4,160,128]{2,1,0:T(8,128)(2,1)S(1)} %get-tuple-element.16), channel_id=1, source_target_pairs={{0,8},{8,0},{1,9},{9,1},{2,10},{10,2},{3,11},{11,3},{4,12},{12,4},... | collective-permute-start | bytes 491528 | tf_op jit(solution)/shard_map/ppermute | solution.py:290
  88.7 13.0 %all-to-all-start.2 = ((bf16[16,40,128]{2,1,0:T(8,128)(2,1)}), bf16[16,40,128]{2,1,0:T(8,128)(2,1)S(1)}, u32[]{:S(2)}, u32[]{:S(2)}) async-start(bf16[16,40,128]{2,1,0:T(8,128)(2,1)} %bitcast.8), calls=%async_computation.2 | async-start | bytes 327680 | tf_op jit(solution)/shard_map/all_to_all | solution.py:285

commit v6 on v5

--- a/solution.py
+++ b/solution.py
@@ -27,6 +27,7 @@
 GAIN = LN2 * LN2 / 3.0 * math.exp(1.5)
 
 COL_STEP = 256
+UNIT = 640
 
 
 VMEM = pl.BlockSpec(memory_space=pltpu.VMEM)
@@ -163,12 +164,13 @@
     return ((arg * arg + REST) * jnp.exp2(arg)).astype(jnp.bfloat16)
 
 
-def tile_kernel(n_sources, skip_own, unroll, own, *refs):
+def tile_kernel(n_sources, skip_own, own, *refs):
     sources, (weights, factors), given = refs[:n_sources], refs[n_sources : n_sources + 2], refs[n_sources + 2 : -5]
     out, held, spread, sums, arrived = refs[-5:]
     n_cols = weights.shape[1]
     n_tasks = factors.shape[0]
     n_rhs = LANES // n_tasks
+    n_rows = held.shape[0]
 
     at, copies = 0, []
     for source in sources:
@@ -191,21 +193,28 @@
     parts = [jnp.where(label == float(task), vectors, 0.0) for task in range(n_tasks)]
     spread[...] = jnp.concatenate(parts, axis=0).astype(jnp.bfloat16)
 
-    def group(index, carry):
-        for sub in range(unroll):
-            col = pl.multiple_of((index * unroll + sub) * COL_STEP, COL_STEP)
-            left = held[...]
-            found = jnp.dot(
-                jnp.concatenate([left, left], axis=1),
-                weights[:, pl.ds(col, COL_STEP)],
-                preferred_element_type=jnp.float32,
+    def distances(unit, col):
+        left = held[unit * UNIT : (unit + 1) * UNIT]
+        return jnp.dot(
+            jnp.concatenate([left, left], axis=1),
+            weights[:, col : col + COL_STEP],
+            preferred_element_type=jnp.float32,
+        )
+
+    n_units = n_rows // UNIT
+    units = [(unit, col) for col in range(0, n_cols, COL_STEP) for unit in range(n_units)]
+    ahead = distances(*units[0])
+    done = []
+    for index, (unit, col) in enumerate(units):
+        now = ahead
+        if index + 1 < len(units):
+            ahead = distances(*units[index + 1])
+        done.append(shaped(now))
+        if unit == n_units - 1:
+            sums[:, col : col + COL_STEP] = jnp.dot(
+                spread[...], jnp.concatenate(done, axis=0), preferred_element_type=jnp.float32
             )
-            sums[:, pl.ds(col, COL_STEP)] = jnp.dot(
-                spread[...], shaped(found), preferred_element_type=jnp.float32
-            )
-        return carry
-
-    lax.fori_loop(0, n_cols // COL_STEP // unroll, group, 0)
+            done = []
 
     wide = n_cols // GROUPS
     stacked = []
@@ -224,11 +233,11 @@
     out[...] = result.astype(out.dtype)
 
 
-def tile(sources, own, weights, factors, given, skip_own, unroll, out_dtype=jnp.float32):
+def tile(sources, own, weights, factors, given, skip_own, out_dtype=jnp.float32):
     n_cols = weights.shape[1]
     n_rows = sum((s.shape[0] - (1 if skip_own else 0)) * s.shape[1] for s in sources)
     return pl.pallas_call(
-        functools.partial(tile_kernel, len(sources), skip_own, unroll),
+        functools.partial(tile_kernel, len(sources), skip_own),
         out_shape=pltpu.VMEM((n_cols // GROUPS, LANES), out_dtype),
         in_specs=[SMEM] + [ANY] * len(sources) + [VMEM] * (2 + len(given)),
         out_specs=VMEM,
@@ -302,10 +311,10 @@
     all_rows = exchange(copies, NEAR)
     weights, factors = weigh(cols, coregion)
     first = [value.reshape(1, -1, LANES) for value in (rows, twin)]
-    total = tile(first, own, weights, factors, [], False, 10)
+    total = tile(first, own, weights, factors, [], False)
     twins = from_shift(all_rows, "core", 1)
-    total = tile([all_rows], own, weights, factors, [total], True, 10)
-    total = tile([twins], own, weights, factors, [total], True, 10, jnp.bfloat16)
+    total = tile([all_rows], own, weights, factors, [total], True)
+    total = tile([twins], own, weights, factors, [total], True, jnp.bfloat16)
     back = exchange(total.reshape(across, -1, LANES), COLS)
     return finish(back, rhs.T, noise).T
 

time: 104 us -> 103 us (level)
  Pallas kernels: 30.1 us -> 28.8 us
    pallas_call x3, Pallas kernels: 25.5 us -> 24.2 us  [tile(): pl.pallas_call(functools.partial(tile_kernel, len(sources), skip_own), ou...]
  transfers between devices with their start and end apart: 7 -> 7, of which waited for: 4 -> 4; matrix products, arithmetic and copies ran while one was open for 0% -> 0% of each run, Pallas kernels for 16% -> 15%
where the time goes in v6:
time: 103 us; the launch traced here: 102 us
  starting transfers between devices  42.3 us (41%)
  Pallas kernels  28.8 us (28%)
  waiting for transfers between devices  16.6 us (16%)
  blocking collectives  13.5 us (13%)
    ppermute x5, starting transfers between devices, from_shift(): lax.ppermute(value, axis, [(i, (i + shift) % count) for i in range(count)])  29.8 us
    pallas_call x3, Pallas kernels, tile(): pl.pallas_call(functools.partial(tile_kernel, len(sources), skip_own), ou...  24.2 us
    all_to_all x1, blocking collectives, exchange(): return lax.all_to_all(blocks, axes, 0, 0, tiled=True)  13.5 us
    all_to_all x2, starting transfers between devices, exchange(): return lax.all_to_all(blocks, axes, 0, 0, tiled=True)  12.5 us
    all_to_all x2, waiting for transfers between devices, exchange(): return lax.all_to_all(blocks, axes, 0, 0, tiled=True)  12.3 us
    ppermute x5, waiting for transfers between devices, from_shift(): lax.ppermute(value, axis, [(i, (i + shift) % count) for i in range(count)])  4.34 us
  transfers between devices with their start and end apart: 7, of which 4 were waited for; matrix products, arithmetic and copies ran while one was open for 0% of the time, Pallas kernels for 15%

profile of v6, /device:TPU:2, one launch (start us, length us, event | category | flops | bytes accessed | tf_op | source)
XLA Modules:
  0.0 101.9 jit_solution(7002187892878975469)
XLA Ops:
  0.0 1.9 %pack.1 = (bf16[160,128]{1,0:T(8,128)(2,1)S(1)}, bf16[16,88,128]{2,1,0:T(8,128)(2,1)}) custom-call(s32[1]{0:T(128)} %bitcast.1.at_ref, bf16[64,160]{1,0:T(8,128)(2,1)} %bitcast.14, bf16[32,160]{1,0:T(8,128)(2,1)} %bitcast.12, s32[1,160]{1,0:T(1,128)} %bitcast.15, f32[1,64]{1,0:T(1,128)} %bitcast.16), custom_call_target="tpu_custom_call" | custom-call | tf_op jit(solution)/shard_map/pack/pallas_call | solution.py:84
  1.9 15.7 %collective-permute-start = (bf16[160,128]{1,0:T(8,128)(2,1)S(1)}, bf16[160,128]{1,0:T(8,128)(2,1)S(1)}, u32[]{:S(2)}, u32[]{:S(2)}) collective-permute-start(bf16[160,128]{1,0:T(8,128)(2,1)S(1)} %get-tuple-element.11.refs_0_), channel_id=1, source_target_pairs={{0,256},{128,384},{256,0},{384,128},{1,257},{129,385},{257,1},{385... | collective-permute-start | bytes 122888 | tf_op jit(solution)/shard_map/ppermute | solution.py:299
  17.6 4.3 %collective-permute-start.1 = (bf16[160,128]{1,0:T(8,128)(2,1)S(1)}, bf16[160,128]{1,0:T(8,128)(2,1)S(1)}, u32[]{:S(2)}, u32[]{:S(2)}) collective-permute-start(bf16[160,128]{1,0:T(8,128)(2,1)S(1)} %get-tuple-element.11.refs_0_), channel_id=1, source_target_pairs={{0,128},{128,256},{256,384},{384,0},{1,129},{129,257},{257,385},{3... | collective-permute-start | bytes 122888 | tf_op jit(solution)/shard_map/ppermute | solution.py:299
  21.9 5.5 %collective-permute-start.2 = (bf16[160,128]{1,0:T(8,128)(2,1)S(1)}, bf16[160,128]{1,0:T(8,128)(2,1)S(1)}, u32[]{:S(2)}, u32[]{:S(2)}) collective-permute-start(bf16[160,128]{1,0:T(8,128)(2,1)S(1)} %get-tuple-element.11.refs_0_), channel_id=1, source_target_pairs={{0,384},{128,0},{256,128},{384,256},{1,385},{129,1},{257,129},{385... | collective-permute-start | bytes 122888 | tf_op jit(solution)/shard_map/ppermute | solution.py:299
  27.3 0.0 collective-permute-done.refs_1_
  27.3 1.8 %collective-permute-done.1.refs_2_ = bf16[160,128]{1,0:T(8,128)(2,1)S(1)} collective-permute-done((bf16[160,128]{1,0:T(8,128)(2,1)S(1)}, bf16[160,128]{1,0:T(8,128)(2,1)S(1)}, u32[]{:S(2)}, u32[]{:S(2)}) %collective-permute-start.1) | collective-permute-done | bytes 40992 | tf_op jit(solution)/shard_map/ppermute | solution.py:299
  29.1 2.6 %collective-permute-done.2.refs_3_ = bf16[160,128]{1,0:T(8,128)(2,1)S(1)} collective-permute-done((bf16[160,128]{1,0:T(8,128)(2,1)S(1)}, bf16[160,128]{1,0:T(8,128)(2,1)S(1)}, u32[]{:S(2)}, u32[]{:S(2)}) %collective-permute-start.2) | collective-permute-done | bytes 40992 | tf_op jit(solution)/shard_map/ppermute | solution.py:299
  31.7 0.1 join.1
  31.8 13.5 %all_to_all.15.refs_0_ = bf16[4,640,128]{2,1,0:T(8,128)(2,1)} all-to-all(bf16[4,640,128]{2,1,0:T(8,128)(2,1)S(1)} %get-tuple-element.12), channel_id=1, replica_groups=mesh['zh'=4,'zl'=4,'xl'=2,'core'=2,'xh'=2,'y'=4] {'y'}, dimensions={0} | all-to-all | bytes 1310720 | tf_op jit(solution)/shard_map/all_to_all | solution.py:294
  45.3 7.4 %all-to-all-start.1 = ((bf16[16,88,128]{2,1,0:T(8,128)(2,1)}), bf16[16,88,128]{2,1,0:T(8,128)(2,1)S(1)}, u32[]{:S(2)}, u32[]{:S(2)}) async-start(bf16[16,88,128]{2,1,0:T(8,128)(2,1)} %get-tuple-element.13), calls=%async_computation.1 | async-start | bytes 720896 | tf_op jit(solution)/shard_map/all_to_all | solution.py:294
  52.7 1.9 %collective-permute-start.3 = (bf16[4,640,128]{2,1,0:T(8,128)(2,1)}, bf16[4,640,128]{2,1,0:T(8,128)(2,1)}, u32[]{:S(2)}, u32[]{:S(2)}) collective-permute-start(bf16[4,640,128]{2,1,0:T(8,128)(2,1)} %all_to_all.15.refs_0_), channel_id=1, source_target_pairs={{0,8},{8,0},{1,9},{9,1},{2,10},{10,2},{3,11},{11,3},{4,12},{12,4},... | collective-permute-start | bytes 1966088 | tf_op jit(solution)/shard_map/ppermute | solution.py:299
  54.6 2.4 %collective-permute-start.4 = (bf16[4,160,128]{2,1,0:T(8,128)(2,1)S(1)}, bf16[4,160,128]{2,1,0:T(8,128)(2,1)S(1)}, u32[]{:S(2)}, u32[]{:S(2)}) collective-permute-start(bf16[4,160,128]{2,1,0:T(8,128)(2,1)S(1)} %get-tuple-element.16), channel_id=1, source_target_pairs={{0,8},{8,0},{1,9},{9,1},{2,10},{10,2},{3,11},{11,3},{4,12},{12,4},... | collective-permute-start | bytes 491528 | tf_op jit(solution)/shard_map/ppermute | solution.py:299
  57.0 5.1 %all-to-all-done.1.cols = bf16[16,88,128]{2,1,0:T(8,128)(2,1)S(1)} async-done(((bf16[16,88,128]{2,1,0:T(8,128)(2,1)}), bf16[16,88,128]{2,1,0:T(8,128)(2,1)S(1)}, u32[]{:S(2)}, u32[]{:S(2)}) %all-to-all-start.1) | async-done | bytes 360480 | tf_op jit(solution)/shard_map/all_to_all | solution.py:294
  62.1 1.0 %weigh.1 = (bf16[256,2560]{1,0:T(8,128)(2,1)S(1)}, f32[4,2560]{1,0:T(4,128)S(1)}) custom-call(bf16[16,88,128]{2,1,0:T(8,128)(2,1)S(1)} %all-to-all-done.1.cols, f32[4,4]{1,0:T(4,128)} %coregion.1), custom_call_target="tpu_custom_call" | custom-call | tf_op jit(solution)/shard_map/weigh/pallas_call | solution.py:144
  63.2 0.0 collective-permute-done.4
  63.2 5.6 %shard_map.64.refs_3_ = f32[640,128]{1,0:T(8,128)S(1)} custom-call(s32[1]{0:T(128)} %bitcast.own, bf16[1,640,128]{2,1,0:T(8,128)(2,1)S(1)} %bitcast.10, bf16[1,640,128]{2,1,0:T(8,128)(2,1)S(1)} %bitcast.11, bf16[256,2560]{1,0:T(8,128)(2,1)S(1)} %get-tuple-element.14.refs_2_.refs_1_, f32[4,2560]{1,0:T(4,128)S(1)} %get-tuple-element.15.refs_3_.refs_2_), custom_call_target="tpu_custom_call" | custom-call | tf_op jit(solution)/shard_map/pallas_call | solution.py:239
  68.8 9.1 %shard_map.65.refs_3_ = f32[640,128]{1,0:T(8,128)S(1)} custom-call(s32[1]{0:T(128)} %bitcast.own, bf16[4,640,128]{2,1,0:T(8,128)(2,1)} %all_to_all.15.refs_0_, bf16[256,2560]{1,0:T(8,128)(2,1)S(1)} %get-tuple-element.14.refs_2_.refs_1_, f32[4,2560]{1,0:T(4,128)S(1)} %get-tuple-element.15.refs_3_.refs_2_, f32[640,128]{1,0:T(8,128)S(1)} %shard_map.64.refs_3_), custom_call_target="tpu_custom_call" | custom-call | tf_op jit(solution)/shard_map/pallas_call | solution.py:239
  77.9 0.0 collective-permute-done.3.refs_0_
  77.9 9.6 %shard_map.66 = bf16[640,128]{1,0:T(8,128)(2,1)} custom-call(s32[1]{0:T(128)} %bitcast.own, bf16[4,640,128]{2,1,0:T(8,128)(2,1)} %collective-permute-done.3.refs_0_, bf16[256,2560]{1,0:T(8,128)(2,1)S(1)} %get-tuple-element.14.refs_2_.refs_1_, f32[4,2560]{1,0:T(4,128)S(1)} %get-tuple-element.15.refs_3_.refs_2_, f32[640,128]{1,0:T(8,128)S(1)} %shard_map.65.refs_3_), custom_call_target="tpu_custom_call" | custom-call | tf_op jit(solution)/shard_map/pallas_call | solution.py:239
  87.4 5.1 %all-to-all-start.2 = ((bf16[16,40,128]{2,1,0:T(8,128)(2,1)}), bf16[16,40,128]{2,1,0:T(8,128)(2,1)S(1)}, u32[]{:S(2)}, u32[]{:S(2)}) async-start(bf16[16,40,128]{2,1,0:T(8,128)(2,1)} %bitcast.8), calls=%async_computation.2 | async-start | bytes 327680 | tf_op jit(solution)/shard_map/all_to_all | solution.py:294
  93.2 7.2 %all-to-all-done.2.parts = bf16[16,40,128]{2,1,0:T(8,128)(2,1)S(1)} async-done(((bf16[16,40,128]{2,1,0:T(8,128)(2,1)}), bf16[16,40,128]{2,1,0:T(8,128)(2,1)S(1)}, u32[]{:S(2)}, u32[]{:S(2)}) %all-to-all-start.2) | async-done | bytes 163872 | tf_op jit(solution)/shard_map/all_to_all | solution.py:294
  100.4 1.5 %finish.1 = f32[32,160]{1,0:T(8,128)} custom-call(bf16[16,40,128]{2,1,0:T(8,128)(2,1)S(1)} %all-to-all-done.2.parts, bf16[32,160]{1,0:T(8,128)(2,1)} %bitcast.13, f32[1]{0:T(128)S(6)} %copy.7.noise), custom_call_target="tpu_custom_call" | custom-call | tf_op jit(solution)/shard_map/finish/pallas_call | solution.py:284
Async XLA Ops:
  1.9 25.5 %collective-permute-start = (bf16[160,128]{1,0:T(8,128)(2,1)S(1)}, bf16[160,128]{1,0:T(8,128)(2,1)S(1)}, u32[]{:S(2)}, u32[]{:S(2)}) collective-permute-start(bf16[160,128]{1,0:T(8,128)(2,1)S(1)} %get-tuple-element.11.refs_0_), channel_id=1, source_target_pairs={{0,256},{128,384},{256,0},{384,128},{1,257},{129,385},{257,1},{385... | collective-permute-start | bytes 122888 | tf_op jit(solution)/shard_map/ppermute | solution.py:299
  17.6 11.5 %collective-permute-start.1 = (bf16[160,128]{1,0:T(8,128)(2,1)S(1)}, bf16[160,128]{1,0:T(8,128)(2,1)S(1)}, u32[]{:S(2)}, u32[]{:S(2)}) collective-permute-start(bf16[160,128]{1,0:T(8,128)(2,1)S(1)} %get-tuple-element.11.refs_0_), channel_id=1, source_target_pairs={{0,128},{128,256},{256,384},{384,0},{1,129},{129,257},{257,385},{3... | collective-permute-start | bytes 122888 | tf_op jit(solution)/shard_map/ppermute | solution.py:299
  21.9 9.8 %collective-permute-start.2 = (bf16[160,128]{1,0:T(8,128)(2,1)S(1)}, bf16[160,128]{1,0:T(8,128)(2,1)S(1)}, u32[]{:S(2)}, u32[]{:S(2)}) collective-permute-start(bf16[160,128]{1,0:T(8,128)(2,1)S(1)} %get-tuple-element.11.refs_0_), channel_id=1, source_target_pairs={{0,384},{128,0},{256,128},{384,256},{1,385},{129,1},{257,129},{385... | collective-permute-start | bytes 122888 | tf_op jit(solution)/shard_map/ppermute | solution.py:299
  45.3 16.8 %all-to-all-start.1 = ((bf16[16,88,128]{2,1,0:T(8,128)(2,1)}), bf16[16,88,128]{2,1,0:T(8,128)(2,1)S(1)}, u32[]{:S(2)}, u32[]{:S(2)}) async-start(bf16[16,88,128]{2,1,0:T(8,128)(2,1)} %get-tuple-element.13), calls=%async_computation.1 | async-start | bytes 720896 | tf_op jit(solution)/shard_map/all_to_all | solution.py:294
  52.7 25.2 %collective-permute-start.3 = (bf16[4,640,128]{2,1,0:T(8,128)(2,1)}, bf16[4,640,128]{2,1,0:T(8,128)(2,1)}, u32[]{:S(2)}, u32[]{:S(2)}) collective-permute-start(bf16[4,640,128]{2,1,0:T(8,128)(2,1)} %all_to_all.15.refs_0_), channel_id=1, source_target_pairs={{0,8},{8,0},{1,9},{9,1},{2,10},{10,2},{3,11},{11,3},{4,12},{12,4},... | collective-permute-start | bytes 1966088 | tf_op jit(solution)/shard_map/ppermute | solution.py:299
  54.6 8.5 %collective-permute-start.4 = (bf16[4,160,128]{2,1,0:T(8,128)(2,1)S(1)}, bf16[4,160,128]{2,1,0:T(8,128)(2,1)S(1)}, u32[]{:S(2)}, u32[]{:S(2)}) collective-permute-start(bf16[4,160,128]{2,1,0:T(8,128)(2,1)S(1)} %get-tuple-element.16), channel_id=1, source_target_pairs={{0,8},{8,0},{1,9},{9,1},{2,10},{10,2},{3,11},{11,3},{4,12},{12,4},... | collective-permute-start | bytes 491528 | tf_op jit(solution)/shard_map/ppermute | solution.py:299
  87.4 13.0 %all-to-all-start.2 = ((bf16[16,40,128]{2,1,0:T(8,128)(2,1)}), bf16[16,40,128]{2,1,0:T(8,128)(2,1)S(1)}, u32[]{:S(2)}, u32[]{:S(2)}) async-start(bf16[16,40,128]{2,1,0:T(8,128)(2,1)} %bitcast.8), calls=%async_computation.2 | async-start | bytes 327680 | tf_op jit(solution)/shard_map/all_to_all | solution.py:294

commit v7 on v6

--- a/solution.py
+++ b/solution.py
@@ -27,7 +27,6 @@
 GAIN = LN2 * LN2 / 3.0 * math.exp(1.5)
 
 COL_STEP = 256
-UNIT = 640
 
 
 VMEM = pl.BlockSpec(memory_space=pltpu.VMEM)
@@ -194,14 +193,15 @@
     spread[...] = jnp.concatenate(parts, axis=0).astype(jnp.bfloat16)
 
     def distances(unit, col):
-        left = held[unit * UNIT : (unit + 1) * UNIT]
+        left = held[unit * size : (unit + 1) * size]
         return jnp.dot(
             jnp.concatenate([left, left], axis=1),
             weights[:, col : col + COL_STEP],
             preferred_element_type=jnp.float32,
         )
 
-    n_units = n_rows // UNIT
+    n_units = 2
+    size = n_rows // n_units
     units = [(unit, col) for col in range(0, n_cols, COL_STEP) for unit in range(n_units)]
     ahead = distances(*units[0])
     done = []
@@ -287,7 +287,7 @@
         in_specs=[VMEM, VMEM, SMEM],
         out_specs=VMEM,
         name="finish",
-    )(hold(parts), rhs, noise)
+    )(hold(parts), hold(rhs), noise)
 
 
 def exchange(blocks, axes):
@@ -304,7 +304,8 @@
     at = lax.axis_index(COLS)[None].astype(jnp.int32)
     own = lax.axis_index(NEAR)[None].astype(jnp.int32)
     own_rows, own_cols = pack(at, points.T, rhs.T, task_ids, length_scales, across)
-    others = [from_shift(own_rows, FAR, shift) for shift in (far // 2, 1, far - 1)]
+    others = [from_shift(own_rows, FAR, far // 2)]
+    others += [from_shift(own_rows, FAR, shift) for shift in (1, far - 1)]
     cols = exchange(own_cols, COLS)
     rows, copies = join([own_rows] + others, near)
     twin = from_shift(rows, "core", 1)

time: 103 us -> 101 us (0.981)
  Pallas kernels: 28.8 us -> 27.5 us
where the time goes in v7:
time: 101 us
  starting transfers between devices  42.3 us (42%)
  Pallas kernels  27.5 us (27%)
  waiting for transfers between devices  16.6 us (16%)
  blocking collectives  13.5 us (13%)
    ppermute x5, starting transfers between devices, from_shift(): lax.ppermute(value, axis, [(i, (i + shift) % count) for i in range(count)])  29.8 us
    pallas_call x3, Pallas kernels, tile(): pl.pallas_call(functools.partial(tile_kernel, len(sources), skip_own), ou...  23.7 us
    all_to_all x1, blocking collectives, exchange(): return lax.all_to_all(blocks, axes, 0, 0, tiled=True)  13.5 us
    all_to_all x2, starting transfers between devices, exchange(): return lax.all_to_all(blocks, axes, 0, 0, tiled=True)  12.5 us
    all_to_all x2, waiting for transfers between devices, exchange(): return lax.all_to_all(blocks, axes, 0, 0, tiled=True)  12.3 us
    ppermute x5, waiting for transfers between devices, from_shift(): lax.ppermute(value, axis, [(i, (i + shift) % count) for i in range(count)])  4.34 us
  transfers between devices with their start and end apart: 7, of which 4 were waited for; matrix products, arithmetic and copies ran while one was open for 0% of the time, Pallas kernels for 15%

profile of v7, /device:TPU:2, one launch (start us, length us, event | category | flops | bytes accessed | tf_op | source)
XLA Modules:
  0.0 100.7 jit_solution(14857557134555857127)
XLA Ops:
  0.0 1.9 %pack.1 = (bf16[160,128]{1,0:T(8,128)(2,1)S(1)}, bf16[16,88,128]{2,1,0:T(8,128)(2,1)}) custom-call(s32[1]{0:T(128)} %bitcast.1.at_ref, bf16[64,160]{1,0:T(8,128)(2,1)} %bitcast.14, bf16[32,160]{1,0:T(8,128)(2,1)} %bitcast.12, s32[1,160]{1,0:T(1,128)} %bitcast.15, f32[1,64]{1,0:T(1,128)} %bitcast.16), custom_call_target="tpu_custom_call" | custom-call | tf_op jit(solution)/shard_map/pack/pallas_call | solution.py:83
  1.9 15.7 %collective-permute-start = (bf16[160,128]{1,0:T(8,128)(2,1)S(1)}, bf16[160,128]{1,0:T(8,128)(2,1)S(1)}, u32[]{:S(2)}, u32[]{:S(2)}) collective-permute-start(bf16[160,128]{1,0:T(8,128)(2,1)S(1)} %get-tuple-element.11.refs_0_), channel_id=1, source_target_pairs={{0,256},{128,384},{256,0},{384,128},{1,257},{129,385},{257,1},{385... | collective-permute-start | bytes 122888 | tf_op jit(solution)/shard_map/ppermute | solution.py:299
  17.6 4.3 %collective-permute-start.1 = (bf16[160,128]{1,0:T(8,128)(2,1)S(1)}, bf16[160,128]{1,0:T(8,128)(2,1)S(1)}, u32[]{:S(2)}, u32[]{:S(2)}) collective-permute-start(bf16[160,128]{1,0:T(8,128)(2,1)S(1)} %get-tuple-element.11.refs_0_), channel_id=1, source_target_pairs={{0,128},{128,256},{256,384},{384,0},{1,129},{129,257},{257,385},{3... | collective-permute-start | bytes 122888 | tf_op jit(solution)/shard_map/ppermute | solution.py:299
  21.9 5.5 %collective-permute-start.2 = (bf16[160,128]{1,0:T(8,128)(2,1)S(1)}, bf16[160,128]{1,0:T(8,128)(2,1)S(1)}, u32[]{:S(2)}, u32[]{:S(2)}) collective-permute-start(bf16[160,128]{1,0:T(8,128)(2,1)S(1)} %get-tuple-element.11.refs_0_), channel_id=1, source_target_pairs={{0,384},{128,0},{256,128},{384,256},{1,385},{129,1},{257,129},{385... | collective-permute-start | bytes 122888 | tf_op jit(solution)/shard_map/ppermute | solution.py:299
  27.3 0.0 collective-permute-done.refs_1_
  27.4 1.8 %collective-permute-done.1.refs_2_ = bf16[160,128]{1,0:T(8,128)(2,1)S(1)} collective-permute-done((bf16[160,128]{1,0:T(8,128)(2,1)S(1)}, bf16[160,128]{1,0:T(8,128)(2,1)S(1)}, u32[]{:S(2)}, u32[]{:S(2)}) %collective-permute-start.1) | collective-permute-done | bytes 40992 | tf_op jit(solution)/shard_map/ppermute | solution.py:299
  29.1 2.6 %collective-permute-done.2.refs_3_ = bf16[160,128]{1,0:T(8,128)(2,1)S(1)} collective-permute-done((bf16[160,128]{1,0:T(8,128)(2,1)S(1)}, bf16[160,128]{1,0:T(8,128)(2,1)S(1)}, u32[]{:S(2)}, u32[]{:S(2)}) %collective-permute-start.2) | collective-permute-done | bytes 40992 | tf_op jit(solution)/shard_map/ppermute | solution.py:299
  31.7 0.1 join.1
  31.8 13.5 %all_to_all.15.refs_0_ = bf16[4,640,128]{2,1,0:T(8,128)(2,1)} all-to-all(bf16[4,640,128]{2,1,0:T(8,128)(2,1)S(1)} %get-tuple-element.12), channel_id=1, replica_groups=mesh['zh'=4,'zl'=4,'xl'=2,'core'=2,'xh'=2,'y'=4] {'y'}, dimensions={0} | all-to-all | bytes 1310720 | tf_op jit(solution)/shard_map/all_to_all | solution.py:294
  45.3 7.4 %all-to-all-start.1 = ((bf16[16,88,128]{2,1,0:T(8,128)(2,1)}), bf16[16,88,128]{2,1,0:T(8,128)(2,1)S(1)}, u32[]{:S(2)}, u32[]{:S(2)}) async-start(bf16[16,88,128]{2,1,0:T(8,128)(2,1)} %get-tuple-element.13), calls=%async_computation.1 | async-start | bytes 720896 | tf_op jit(solution)/shard_map/all_to_all | solution.py:294
  52.7 1.9 %collective-permute-start.3 = (bf16[4,640,128]{2,1,0:T(8,128)(2,1)}, bf16[4,640,128]{2,1,0:T(8,128)(2,1)}, u32[]{:S(2)}, u32[]{:S(2)}) collective-permute-start(bf16[4,640,128]{2,1,0:T(8,128)(2,1)} %all_to_all.15.refs_0_), channel_id=1, source_target_pairs={{0,8},{8,0},{1,9},{9,1},{2,10},{10,2},{3,11},{11,3},{4,12},{12,4},... | collective-permute-start | bytes 1966088 | tf_op jit(solution)/shard_map/ppermute | solution.py:299
  54.6 2.4 %collective-permute-start.4 = (bf16[4,160,128]{2,1,0:T(8,128)(2,1)S(1)}, bf16[4,160,128]{2,1,0:T(8,128)(2,1)S(1)}, u32[]{:S(2)}, u32[]{:S(2)}) collective-permute-start(bf16[4,160,128]{2,1,0:T(8,128)(2,1)S(1)} %get-tuple-element.16), channel_id=1, source_target_pairs={{0,8},{8,0},{1,9},{9,1},{2,10},{10,2},{3,11},{11,3},{4,12},{12,4},... | collective-permute-start | bytes 491528 | tf_op jit(solution)/shard_map/ppermute | solution.py:299
  57.0 5.1 %all-to-all-done.1.cols = bf16[16,88,128]{2,1,0:T(8,128)(2,1)S(1)} async-done(((bf16[16,88,128]{2,1,0:T(8,128)(2,1)}), bf16[16,88,128]{2,1,0:T(8,128)(2,1)S(1)}, u32[]{:S(2)}, u32[]{:S(2)}) %all-to-all-start.1) | async-done | bytes 360480 | tf_op jit(solution)/shard_map/all_to_all | solution.py:294
  62.1 1.0 %weigh.1 = (bf16[256,2560]{1,0:T(8,128)(2,1)S(1)}, f32[4,2560]{1,0:T(4,128)S(1)}) custom-call(bf16[16,88,128]{2,1,0:T(8,128)(2,1)S(1)} %all-to-all-done.1.cols, f32[4,4]{1,0:T(4,128)} %coregion.1), custom_call_target="tpu_custom_call" | custom-call | tf_op jit(solution)/shard_map/weigh/pallas_call | solution.py:143
  63.2 0.0 collective-permute-done.4
  63.2 5.6 %shard_map.64.refs_3_ = f32[640,128]{1,0:T(8,128)S(1)} custom-call(s32[1]{0:T(128)} %bitcast.own, bf16[1,640,128]{2,1,0:T(8,128)(2,1)S(1)} %bitcast.10, bf16[1,640,128]{2,1,0:T(8,128)(2,1)S(1)} %bitcast.11, bf16[256,2560]{1,0:T(8,128)(2,1)S(1)} %get-tuple-element.14.refs_2_.refs_1_, f32[4,2560]{1,0:T(4,128)S(1)} %get-tuple-element.15.refs_3_.refs_2_), custom_call_target="tpu_custom_call" | custom-call | tf_op jit(solution)/shard_map/pallas_call | solution.py:239
  68.8 8.8 %shard_map.65.refs_3_ = f32[640,128]{1,0:T(8,128)S(1)} custom-call(s32[1]{0:T(128)} %bitcast.own, bf16[4,640,128]{2,1,0:T(8,128)(2,1)} %all_to_all.15.refs_0_, bf16[256,2560]{1,0:T(8,128)(2,1)S(1)} %get-tuple-element.14.refs_2_.refs_1_, f32[4,2560]{1,0:T(4,128)S(1)} %get-tuple-element.15.refs_3_.refs_2_, f32[640,128]{1,0:T(8,128)S(1)} %shard_map.64.refs_3_), custom_call_target="tpu_custom_call" | custom-call | tf_op jit(solution)/shard_map/pallas_call | solution.py:239
  77.6 0.0 copy-start
  77.6 0.0 collective-permute-done.3.refs_0_
  77.6 9.3 %shard_map.66 = bf16[640,128]{1,0:T(8,128)(2,1)} custom-call(s32[1]{0:T(128)} %bitcast.own, bf16[4,640,128]{2,1,0:T(8,128)(2,1)} %collective-permute-done.3.refs_0_, bf16[256,2560]{1,0:T(8,128)(2,1)S(1)} %get-tuple-element.14.refs_2_.refs_1_, f32[4,2560]{1,0:T(4,128)S(1)} %get-tuple-element.15.refs_3_.refs_2_, f32[640,128]{1,0:T(8,128)S(1)} %shard_map.65.refs_3_), custom_call_target="tpu_custom_call" | custom-call | tf_op jit(solution)/shard_map/pallas_call | solution.py:239
  86.9 5.1 %all-to-all-start.2 = ((bf16[16,40,128]{2,1,0:T(8,128)(2,1)}), bf16[16,40,128]{2,1,0:T(8,128)(2,1)S(1)}, u32[]{:S(2)}, u32[]{:S(2)}) async-start(bf16[16,40,128]{2,1,0:T(8,128)(2,1)} %bitcast.8), calls=%async_computation.2 | async-start | bytes 327680 | tf_op jit(solution)/shard_map/all_to_all | solution.py:294
  92.7 7.2 %all-to-all-done.2.parts = bf16[16,40,128]{2,1,0:T(8,128)(2,1)S(1)} async-done(((bf16[16,40,128]{2,1,0:T(8,128)(2,1)}), bf16[16,40,128]{2,1,0:T(8,128)(2,1)S(1)}, u32[]{:S(2)}, u32[]{:S(2)}) %all-to-all-start.2) | async-done | bytes 163872 | tf_op jit(solution)/shard_map/all_to_all | solution.py:294
  99.9 0.0 copy-done
  99.9 0.8 finish.1
Async XLA Ops:
  1.9 25.5 %collective-permute-start = (bf16[160,128]{1,0:T(8,128)(2,1)S(1)}, bf16[160,128]{1,0:T(8,128)(2,1)S(1)}, u32[]{:S(2)}, u32[]{:S(2)}) collective-permute-start(bf16[160,128]{1,0:T(8,128)(2,1)S(1)} %get-tuple-element.11.refs_0_), channel_id=1, source_target_pairs={{0,256},{128,384},{256,0},{384,128},{1,257},{129,385},{257,1},{385... | collective-permute-start | bytes 122888 | tf_op jit(solution)/shard_map/ppermute | solution.py:299
  17.6 11.5 %collective-permute-start.1 = (bf16[160,128]{1,0:T(8,128)(2,1)S(1)}, bf16[160,128]{1,0:T(8,128)(2,1)S(1)}, u32[]{:S(2)}, u32[]{:S(2)}) collective-permute-start(bf16[160,128]{1,0:T(8,128)(2,1)S(1)} %get-tuple-element.11.refs_0_), channel_id=1, source_target_pairs={{0,128},{128,256},{256,384},{384,0},{1,129},{129,257},{257,385},{3... | collective-permute-start | bytes 122888 | tf_op jit(solution)/shard_map/ppermute | solution.py:299
  21.9 9.8 %collective-permute-start.2 = (bf16[160,128]{1,0:T(8,128)(2,1)S(1)}, bf16[160,128]{1,0:T(8,128)(2,1)S(1)}, u32[]{:S(2)}, u32[]{:S(2)}) collective-permute-start(bf16[160,128]{1,0:T(8,128)(2,1)S(1)} %get-tuple-element.11.refs_0_), channel_id=1, source_target_pairs={{0,384},{128,0},{256,128},{384,256},{1,385},{129,1},{257,129},{385... | collective-permute-start | bytes 122888 | tf_op jit(solution)/shard_map/ppermute | solution.py:299
  45.3 16.8 %all-to-all-start.1 = ((bf16[16,88,128]{2,1,0:T(8,128)(2,1)}), bf16[16,88,128]{2,1,0:T(8,128)(2,1)S(1)}, u32[]{:S(2)}, u32[]{:S(2)}) async-start(bf16[16,88,128]{2,1,0:T(8,128)(2,1)} %get-tuple-element.13), calls=%async_computation.1 | async-start | bytes 720896 | tf_op jit(solution)/shard_map/all_to_all | solution.py:294
  52.7 24.9 %collective-permute-start.3 = (bf16[4,640,128]{2,1,0:T(8,128)(2,1)}, bf16[4,640,128]{2,1,0:T(8,128)(2,1)}, u32[]{:S(2)}, u32[]{:S(2)}) collective-permute-start(bf16[4,640,128]{2,1,0:T(8,128)(2,1)} %all_to_all.15.refs_0_), channel_id=1, source_target_pairs={{0,8},{8,0},{1,9},{9,1},{2,10},{10,2},{3,11},{11,3},{4,12},{12,4},... | collective-permute-start | bytes 1966088 | tf_op jit(solution)/shard_map/ppermute | solution.py:299
  54.6 8.5 %collective-permute-start.4 = (bf16[4,160,128]{2,1,0:T(8,128)(2,1)S(1)}, bf16[4,160,128]{2,1,0:T(8,128)(2,1)S(1)}, u32[]{:S(2)}, u32[]{:S(2)}) collective-permute-start(bf16[4,160,128]{2,1,0:T(8,128)(2,1)S(1)} %get-tuple-element.16), channel_id=1, source_target_pairs={{0,8},{8,0},{1,9},{9,1},{2,10},{10,2},{3,11},{11,3},{4,12},{12,4},... | collective-permute-start | bytes 491528 | tf_op jit(solution)/shard_map/ppermute | solution.py:299
  77.6 22.3 %copy-start = (bf16[160,32]{0,1:T(8,128)(2,1)S(1)}, bf16[160,32]{0,1:T(8,128)(2,1)}, u32[]{:S(2)}) copy-start(bf16[160,32]{0,1:T(8,128)(2,1)} %param.8) | copy-start | bytes 30724
  86.9 13.0 %all-to-all-start.2 = ((bf16[16,40,128]{2,1,0:T(8,128)(2,1)}), bf16[16,40,128]{2,1,0:T(8,128)(2,1)S(1)}, u32[]{:S(2)}, u32[]{:S(2)}) async-start(bf16[16,40,128]{2,1,0:T(8,128)(2,1)} %bitcast.8), calls=%async_computation.2 | async-start | bytes 327680 | tf_op jit(solution)/shard_map/all_to_all | solution.py:294
